TPU v7x, 128 devices: a whole 4x4x4 slice. The times are simulated.
128 devices in a mesh: row: 8 (over x, core), col: 16 (over z, y).
Axes of the slice: x: 4, y: 4, z: 4, core: 2. Of those that a mesh axis runs over, the one named last changes fastest.
Arguments:
- concentration: float32 [256, 256, 256], P('row', 'col'), may hold values from 0 to 1
Outputs:
- concentration_next: float32 [256, 256, 256], P('row', 'col')
- strain: float32 [6, 256, 256, 256], P(None, 'row', 'col')
- residual_norms: float32 [2], replicated
All inputs are finite; a program needn't handle non-finite values.
Results may differ from a plain program's by a relative error of at most 0.0003.
Values sent between devices are 32-bit elements; how exact they have to be, the bound alone decides.
A program may use at most 192 MiB of HBM per device.

v0:
```python
import math

import jax
import jax.numpy as jnp
from jax import lax
from jax.sharding import Mesh
from jax.sharding import PartitionSpec as P

ITERS = 2
COL = ("col_0", "col_1")
ROW = ("row_0", "row_1")
ROW_COL = ("row_0", "row_1", "col_0", "col_1")


FIRST_LOW = 1.0
FIRST_RISE = 0.6
SHEAR_LOW = 0.7
SHEAR_RISE = 0.8
FIRST_REF = 1.3
SHEAR_REF = 1.1
BETA_REF = 2.4 / 3.5
EIGEN_STRAIN = 0.5
WELL_HEIGHT = 1.0
TIME_STEP = 0.5
GRADIENT_ENERGY = 0.5


def one_axis_at_a_time(shard, axes):
    for axis in axes:
        shard = lax.psum(shard, axis)
    return shard


def moduli(conc):
    return (FIRST_LOW + FIRST_RISE * conc, SHEAR_LOW + SHEAR_RISE * conc)


def polarization(strain, conc):
    first, shear = moduli(conc)
    trace = strain[0] + strain[1] + strain[2]
    normal = (first - FIRST_REF) * trace - (3.0 * first + 2.0 * shear) * EIGEN_STRAIN * conc
    excess = 2.0 * (shear - SHEAR_REF)
    return jnp.stack(
        [
            normal + excess * strain[0],
            normal + excess * strain[1],
            normal + excess * strain[2],
            excess * strain[3],
            excess * strain[4],
            excess * strain[5],
        ]
    )


def green_operator(tau, wave_x, wave_y, wave_z):
    square = wave_x * wave_x + wave_y * wave_y + wave_z * wave_z
    nonzero = square > 0.0
    safe = jnp.where(nonzero, square, 1.0)
    scale = jnp.where(nonzero, 1.0 / (SHEAR_REF * safe), 0.0)
    force_x = tau[0] * wave_x + tau[5] * wave_y + tau[4] * wave_z
    force_y = tau[5] * wave_x + tau[1] * wave_y + tau[3] * wave_z
    force_z = tau[4] * wave_x + tau[3] * wave_y + tau[2] * wave_z
    along = (wave_x * force_x + wave_y * force_y + wave_z * force_z) * (BETA_REF / safe)
    moved_x = scale * (force_x - along * wave_x)
    moved_y = scale * (force_y - along * wave_y)
    moved_z = scale * (force_z - along * wave_z)
    return jnp.stack(
        [
            -wave_x * moved_x,
            -wave_y * moved_y,
            -wave_z * moved_z,
            -0.5 * (wave_y * moved_z + wave_z * moved_y),
            -0.5 * (wave_x * moved_z + wave_z * moved_x),
            -0.5 * (wave_x * moved_y + wave_y * moved_x),
        ]
    )


def potential(strain, conc):
    first, shear = moduli(conc)
    dilation = EIGEN_STRAIN * conc
    part_x = strain[0] - dilation
    part_y = strain[1] - dilation
    part_z = strain[2] - dilation
    trace = part_x + part_y + part_z
    energy = (
        part_x * part_x
        + part_y * part_y
        + part_z * part_z
        + 2.0 * (strain[3] * strain[3] + strain[4] * strain[4] + strain[5] * strain[5])
    )
    chemical = 2.0 * WELL_HEIGHT * conc * (1.0 - conc) * (1.0 - 2.0 * conc)
    return (
        chemical
        + 0.5 * FIRST_RISE * trace * trace
        + SHEAR_RISE * energy
        - EIGEN_STRAIN * (3.0 * first + 2.0 * shear) * trace
    )


def build_tables(length):
    index = jnp.arange(length, dtype=jnp.int32)
    product = index[:, None] * index[None, :] % length
    angle = product.astype(jnp.float32) * (2.0 * math.pi / length)
    cosine = jnp.cos(angle)
    sine = jnp.sin(angle)
    half_length = length // 2
    ahead = jnp.stack(
        [jnp.stack([cosine, -sine], axis=1), jnp.stack([sine, cosine], axis=1)], axis=0
    )
    back = (
        jnp.stack([jnp.stack([cosine, sine], axis=1), jnp.stack([-sine, cosine], axis=1)], axis=0)
        / length
    )
    back = back.transpose(0, 1, 3, 2)
    z_ahead = jnp.stack([cosine[:, :half_length], -sine[:, :half_length]], axis=1)
    weight = (jnp.where(jnp.arange(half_length, dtype=jnp.int32) == 0, 1.0, 2.0) / length)[:, None]
    z_back = jnp.stack([cosine[:half_length, :] * weight, -sine[:half_length, :] * weight], axis=0)
    return (ahead, back, z_ahead, z_back)


def signed_waves(index, length):
    shifted = jnp.where(index < length // 2, index, index - length)
    return shifted.astype(jnp.float32) * (2.0 * math.pi / length)


def plain_waves(index, length):
    return index.astype(jnp.float32) * (2.0 * math.pi / length)


def contract(form, data, table):
    return jnp.einsum(
        form, data, table, precision=lax.Precision.HIGHEST, preferred_element_type=jnp.float32
    )


def z_forward(fields, tables):
    members, local_x, local_y, length = fields.shape
    half_length = length // 2
    spectrum = contract("fxyz,zbk->fbkxy", fields, tables[2])
    return spectrum.reshape(members, 2, 1, half_length, local_x * local_y)


def z_inverse(spectrum, tables, local_x, local_y):
    members = spectrum.shape[0]
    half_length = tables[3].shape[1]
    spectrum = spectrum.reshape(members, 2, half_length, local_x, local_y)
    return contract("fakxy,akz->fxyz", spectrum, tables[3])


def forward_col(fields, tables):
    members, local_x, local_y, length = fields.shape
    half_length = length // 2
    spectrum = z_forward(fields, tables)
    spectrum = lax.all_to_all(spectrum, COL, split_axis=3, concat_axis=2, tiled=True)
    ncols = lax.axis_size(COL)
    kz_local = half_length // ncols
    spectrum = spectrum.reshape(members, 2, ncols, kz_local, local_x, local_y)
    spectrum = contract(
        "fackxl,aclbm->fbmkx", spectrum, tables[0].reshape(2, ncols, local_y, 2, length)
    )
    spectrum = spectrum.reshape(members, 2, 1, length, kz_local * local_x)
    spectrum = lax.all_to_all(spectrum, ROW, split_axis=3, concat_axis=2, tiled=True)
    nrows = lax.axis_size(ROW)
    ky_local = length // nrows
    spectrum = spectrum.reshape(members, 2, nrows, ky_local, kz_local, local_x)
    spectrum = contract(
        "farjkx,arxbm->fbjkm", spectrum, tables[0].reshape(2, nrows, local_x, 2, length)
    )
    wave_y = signed_waves(
        lax.axis_index(ROW) * ky_local + jnp.arange(ky_local, dtype=jnp.int32), length
    )[:, None, None]
    wave_z = plain_waves(
        lax.axis_index(COL) * kz_local + jnp.arange(kz_local, dtype=jnp.int32), length
    )[None, :, None]
    wave_x = signed_waves(jnp.arange(length, dtype=jnp.int32), length)[None, None, :]
    return (spectrum, (wave_x, wave_y, wave_z))


def inverse_col(spectrum, tables, local_x, local_y):
    members, parts, ky_local, kz_local, length = spectrum.shape
    nrows = lax.axis_size(ROW)
    ncols = lax.axis_size(COL)
    spectrum = contract(
        "fajkm,amrxb->fbrjkx", spectrum, tables[1].reshape(2, length, nrows, local_x, 2)
    )
    spectrum = spectrum.reshape(members, 2, nrows, ky_local, kz_local * local_x)
    spectrum = lax.all_to_all(spectrum, ROW, split_axis=2, concat_axis=3, tiled=True)
    spectrum = spectrum.reshape(members, 2, length, kz_local, local_x)
    spectrum = contract(
        "fajkx,ajclb->fbckxl", spectrum, tables[1].reshape(2, length, ncols, local_y, 2)
    )
    spectrum = spectrum.reshape(members, 2, ncols, kz_local, local_x * local_y)
    spectrum = lax.all_to_all(spectrum, COL, split_axis=2, concat_axis=3, tiled=True)
    return z_inverse(spectrum, tables, local_x, local_y)


def forward_group(fields, tables):
    return forward_col(fields, tables)


def inverse_group(spectrum, tables, local_x, local_y):
    return inverse_col(spectrum, tables, local_x, local_y)


def forward(fields, tables):
    return forward_group(fields, tables)


def inverse(spectrum, tables, local_x, local_y):
    return inverse_group(spectrum, tables, local_x, local_y)


def shards(concentration):
    local_x, local_y, length = concentration.shape
    tables = build_tables(length)
    strain = jnp.zeros((6, local_x, local_y, length), jnp.float32)
    sums = []
    for sweep in range(ITERS):
        tau = polarization(strain, concentration)
        spectrum, waves = forward(tau, tables)
        spectrum = green_operator(spectrum, waves[0], waves[1], waves[2])
        updated = inverse(spectrum, tables, local_x, local_y)
        change = updated - strain
        partial_sum = jnp.sum(change * change)
        sums.append(one_axis_at_a_time(partial_sum, ROW_COL))
        strain = updated
    totals = jnp.stack(sums)
    residual_norms = jnp.sqrt(totals / length**3)
    drive = potential(strain, concentration)
    spectrum, waves = forward(jnp.stack([concentration, drive]), tables)
    square = waves[0] * waves[0] + waves[1] * waves[1] + waves[2] * waves[2]
    denominator = 1.0 + TIME_STEP * GRADIENT_ENERGY * square * square
    updated_spectrum = (spectrum[0] - TIME_STEP * square * spectrum[1]) / denominator
    concentration_next = inverse(updated_spectrum[None], tables, local_x, local_y)[0]
    return (concentration_next, strain, residual_norms)


def solution(mesh):
    split = Mesh(mesh.devices.reshape(4, 2, 4, 4), ("row_0", "row_1", "col_0", "col_1"))
    in_specs = (P(ROW, COL, None),)
    out_specs = (P(ROW, COL, None), P(None, ROW, COL, None), P())
    return jax.shard_map(
        shards, mesh=split, in_specs=in_specs, out_specs=out_specs, check_vma=False
    )
```

profile of v0, /device:TPU:1, one launch (start us, length us, event | category | flops | bytes accessed | tf_op | source)
XLA Modules:
  0.0 1128.2 jit_solution(896907391976863344)
XLA Ops:
  31.7 45.8 %all-to-all-done = f32[6,2,1,128,512]{4,1,0,2,3:T(2,128)} async-done(((f32[6,2,1,128,512]{4,1,0,2,3:T(2,128)}), f32[6,2,1,128,512]{4,1,0,2,3:T(2,128)}, u32[]{:S(2)}, u32[]{:S(2)}) %all-to-all-start) | async-done | bytes 3145760 | tf_op jit(solution)/shard_map/all_to_all | solution.py:155
  93.4 38.7 %fusion.2 = f32[2,256,6,8,32,1,1]{1,4,6,5,3,2,0:T(8,128)} fusion(f32[1,16,16,1,256]{4,2,1,0,3:T(8,128)S(1)} %get-tuple-element.51, f32[1,16,16,1,256]{4,2,1,0,3:T(8,128)S(1)} %get-tuple-element.50, f32[1,16,16,1,256]{4,2,1,0,3:T(8,128)S(1)} %get-tuple-element.49, f32[6,2,16,8,32,16]{5,4,1,0,3,2:T(8,128)} %reshape.525), kind=kOutput, calls=%fused_computation.2 | convolution fusion | flops 4832624640 | bytes 7077888 | tf_op jit(solution)/shard_map/fackxl,aclbm->fbmkx/dot_general | solution.py:132
  150.1 32.0 %all-to-all-done.1 = f32[6,2,1,256,256]{4,1,0,2,3:T(2,128)} async-done(((f32[6,2,1,256,256]{4,1,0,2,3:T(2,128)}), f32[6,2,1,256,256]{4,1,0,2,3:T(2,128)}, u32[]{:S(2)}, u32[]{:S(2)}) %all-to-all-start.1) | async-done | bytes 3145760 | tf_op jit(solution)/shard_map/all_to_all | solution.py:163
  191.4 26.6 %fusion.41 = f32[6,2,32,8,256]{4,2,3,0,1:T(8,128)S(1)} fusion(f32[6,2,8,32,8,32]{5,4,1,0,3,2:T(8,128)} %reshape.526, f32[1,8,32,1,256]{4,2,1,0,3:T(8,128)S(1)} %get-tuple-element.54, f32[1,8,32,1,256]{4,2,1,0,3:T(8,128)S(1)} %get-tuple-element.53, f32[1,8,32,1,256]{4,2,1,0,3:T(8,128)S(1)} %get-tuple-element.52), kind=kOutput, calls=%fused_computation.39 | convolution fusion | flops 4832624640 | bytes 7077888 | tf_op jit(solution)/shard_map/farjkx,arxbm->fbjkm/dot_general | solution.py:132
  219.8 22.4 %fusion.35 = f32[8,32,2,6,32,8,1]{4,1,6,5,3,2,0:T(8,128)} fusion(f32[2,256,8,32,2,1,1]{1,3,2,4,0,6,5:T(8,128)S(1)} %bitcast.362, f32[6,2,32,8,256]{4,2,3,0,1:T(8,128)S(1)} %multiply_dynamic-update-slice_fusion.6), kind=kOutput, calls=%fused_computation.31 | convolution fusion | flops 4831838208 | bytes 7340032 | tf_op jit(solution)/shard_map/fajkm,amrxb->fbrjkx/dot_general | solution.py:132
  251.0 42.1 %all_to_all.48 = f32[6,2,8,32,256]{4,3,1,0,2:T(8,128)S(1)} all-to-all(f32[6,2,8,32,256]{4,3,1,0,2:T(8,128)} %copy.96), channel_id=1, replica_groups=mesh['row_0'=4,'row_1'=2,'col_0'=4,'col_1'=4] {'row_0','row_1'}, dimensions={2} | all-to-all | bytes 6291456 | tf_op jit(solution)/shard_map/all_to_all | solution.py:188
  303.5 27.1 %fusion.20 = f32[6,2,16,8,32,16]{4,5,3,0,1,2:T(8,128)} fusion(f32[6,2,256,8,32,1,1]{4,3,2,1,0,6,5:T(8,128)} %bitcast.357, f32[2,256,16,16,2,1,1]{1,3,2,4,0,6,5:T(8,128)S(1)} %bitcast.363), kind=kOutput, calls=%fused_computation.20 | convolution fusion | flops 4831838208 | bytes 7340032 | tf_op jit(solution)/shard_map/fajkx,ajclb->fbckxl/dot_general | solution.py:132
  330.6 17.8 %copy.207 = f32[6,2,16,8,32,16]{5,4,3,1,0,2:T(8,128)} copy(f32[6,2,16,8,32,16]{4,5,3,0,1,2:T(8,128)} %fusion.20) | data formatting | bytes 6291456 | tf_op jit(solution)/shard_map/reshape | solution.py:193
  348.4 21.5 %reshape.527 = f32[6,2,16,8,512]{4,3,1,0,2:T(8,128)} reshape(f32[6,2,16,8,32,16]{5,4,3,1,0,2:T(8,128)} %copy.207) | data formatting | bytes 6291456 | tf_op jit(solution)/shard_map/reshape | solution.py:193
  375.1 46.6 %all-to-all-done.3 = f32[6,2,16,8,512]{4,3,1,0,2:T(8,128)} async-done(((f32[6,2,16,8,512]{4,3,1,0,2:T(8,128)}), f32[6,2,16,8,512]{4,3,1,0,2:T(8,128)}, u32[]{:S(2)}, u32[]{:S(2)}) %all-to-all-start.3) | async-done | bytes 3145760 | tf_op jit(solution)/shard_map/all_to_all | solution.py:194
  440.9 50.0 %fusion.47 = f32[6,32,16,256]{3,2,1,0:T(8,128)S(1)} fusion(f32[6,2,128,32,16]{4,3,2,1,0:T(8,128)} %reshape.466, f32[1,128,256]{2,1,0:T(8,128)S(1)} %get-tuple-element.56, f32[1,128,256]{2,1,0:T(8,128)S(1)} %get-tuple-element.55), kind=kOutput, calls=%fused_computation.41 | convolution fusion | flops 2415984640 | bytes 6553600 | tf_op jit(solution)/shard_map/fakxy,akz->fxyz/dot_general | solution.py:132
  509.9 42.9 %all_to_all.49 = f32[6,2,1,128,512]{4,1,0,2,3:T(2,128)} all-to-all(f32[6,2,1,128,512]{4,1,0,2,3:T(2,128)} %copy.111), channel_id=1, replica_groups=mesh['row_0'=4,'row_1'=2,'col_0'=4,'col_1'=4] {'col_0','col_1'}, dimensions={3} | all-to-all | bytes 6291456 | tf_op jit(solution)/shard_map/all_to_all | solution.py:155
  568.8 38.7 %fusion = f32[2,256,6,8,32,1,1]{1,4,6,5,3,2,0:T(8,128)} fusion(f32[1,16,16,1,256]{4,2,1,0,3:T(8,128)S(1)} %copy-done.19, f32[1,16,16,1,256]{4,2,1,0,3:T(8,128)S(1)} %copy-done.16, f32[1,16,16,1,256]{4,2,1,0,3:T(8,128)S(1)} %copy-done.13, f32[6,2,16,8,32,16]{5,4,1,0,3,2:T(8,128)} %reshape.528), kind=kOutput, calls=%fused_computation | convolution fusion | flops 4832624640 | bytes 7077888 | tf_op jit(solution)/shard_map/fackxl,aclbm->fbmkx/dot_general | solution.py:132
  613.3 44.9 %all_to_all.50 = f32[6,2,1,256,256]{4,1,0,2,3:T(2,128)} all-to-all(f32[6,2,1,256,256]{4,1,0,2,3:T(2,128)} %copy.114), channel_id=1, replica_groups=mesh['row_0'=4,'row_1'=2,'col_0'=4,'col_1'=4] {'row_0','row_1'}, dimensions={3} | all-to-all | bytes 6291456 | tf_op jit(solution)/shard_map/all_to_all | solution.py:163
  667.7 26.6 %fusion.44 = f32[6,2,32,8,256]{4,2,3,0,1:T(8,128)S(1)} fusion(f32[6,2,8,32,8,32]{5,4,1,0,3,2:T(8,128)} %reshape.529, f32[1,8,32,1,256]{4,2,1,0,3:T(8,128)S(1)} %copy-done.28, f32[1,8,32,1,256]{4,2,1,0,3:T(8,128)S(1)} %copy-done.25, f32[1,8,32,1,256]{4,2,1,0,3:T(8,128)S(1)} %copy-done.22), kind=kOutput, calls=%fused_computation.40 | convolution fusion | flops 4832624640 | bytes 7077888 | tf_op jit(solution)/shard_map/farjkx,arxbm->fbjkm/dot_general | solution.py:132
  696.0 22.4 %fusion.31 = f32[8,32,2,6,32,8,1]{4,1,6,5,3,2,0:T(8,128)} fusion(f32[2,256,8,32,2,1,1]{1,3,2,4,0,6,5:T(8,128)S(1)} %bitcast.364, f32[6,2,32,8,256]{4,2,3,0,1:T(8,128)S(1)} %multiply_dynamic-update-slice_fusion), kind=kOutput, calls=%fused_computation.27 | convolution fusion | flops 4831838208 | bytes 7340032 | tf_op jit(solution)/shard_map/fajkm,amrxb->fbrjkx/dot_general | solution.py:132
  727.2 42.4 %all_to_all.51 = f32[6,2,8,32,256]{4,3,1,0,2:T(8,128)S(1)} all-to-all(f32[6,2,8,32,256]{4,3,1,0,2:T(8,128)} %copy.119), channel_id=1, replica_groups=mesh['row_0'=4,'row_1'=2,'col_0'=4,'col_1'=4] {'row_0','row_1'}, dimensions={2} | all-to-all | bytes 6291456 | tf_op jit(solution)/shard_map/all_to_all | solution.py:188
  780.1 27.1 %fusion.23 = f32[6,2,16,8,32,16]{4,5,3,0,1,2:T(8,128)} fusion(f32[6,2,256,8,32,1,1]{4,3,2,1,0,6,5:T(8,128)} %bitcast.359, f32[2,256,16,16,2,1,1]{1,3,2,4,0,6,5:T(8,128)S(1)} %bitcast.365), kind=kOutput, calls=%fused_computation.21 | convolution fusion | flops 4831838208 | bytes 7340032 | tf_op jit(solution)/shard_map/fajkx,ajclb->fbckxl/dot_general | solution.py:132
  807.2 17.8 %copy.218 = f32[6,2,16,8,32,16]{5,4,3,1,0,2:T(8,128)} copy(f32[6,2,16,8,32,16]{4,5,3,0,1,2:T(8,128)} %fusion.23) | data formatting | bytes 6291456 | tf_op jit(solution)/shard_map/reshape | solution.py:193
  825.0 21.5 %reshape.530 = f32[6,2,16,8,512]{4,3,1,0,2:T(8,128)} reshape(f32[6,2,16,8,32,16]{5,4,3,1,0,2:T(8,128)} %copy.218) | data formatting | bytes 6291456 | tf_op jit(solution)/shard_map/reshape | solution.py:193
  846.5 42.3 %all_to_all.52 = f32[6,2,16,8,512]{4,3,1,0,2:T(8,128)S(1)} all-to-all(f32[6,2,16,8,512]{4,3,1,0,2:T(8,128)} %reshape.530), channel_id=1, replica_groups=mesh['row_0'=4,'row_1'=2,'col_0'=4,'col_1'=4] {'col_0','col_1'}, dimensions={2} | all-to-all | bytes 6291456 | tf_op jit(solution)/shard_map/all_to_all | solution.py:194
  906.0 58.5 %multiply_reduce_fusion.1 = (f32[]{:T(128)}, f32[]{:T(128)}, f32[6,32,16,256]{3,2,1,0:T(8,128)S(1)}) fusion(f32[6,32,16,256]{3,2,1,0:T(8,128)} %copy-done.1, f32[1,128,256]{2,1,0:T(8,128)S(1)} %get-tuple-element.56, f32[1,128,256]{2,1,0:T(8,128)S(1)} %get-tuple-element.55, f32[6,2,128,32,16]{4,3,2,1,0:T(8,128)} %reshape.474), kind=kOutput, calls=%fused_computation.36 | convolution fusion | flops 2419916800 | bytes 9699336 | tf_op jit(solution)/shard_map/fakxy,akz->fxyz/dot_general | solution.py:132
  971.0 18.7 %all_to_all.53 = f32[2,2,1,128,512]{4,1,0,2,3:T(2,128)S(1)} all-to-all(f32[2,2,1,128,512]{4,1,0,2,3:T(2,128)S(1)} %copy.135), channel_id=1, replica_groups=mesh['row_0'=4,'row_1'=2,'col_0'=4,'col_1'=4] {'col_0','col_1'}, dimensions={3} | all-to-all | bytes 2097152 | tf_op jit(solution)/shard_map/all_to_all | solution.py:155
  1009.4 20.3 %all_to_all.54 = f32[2,2,1,256,256]{4,1,0,2,3:T(2,128)S(1)} all-to-all(f32[2,2,1,256,256]{4,1,0,2,3:T(2,128)S(1)} %copy.138), channel_id=1, replica_groups=mesh['row_0'=4,'row_1'=2,'col_0'=4,'col_1'=4] {'row_0','row_1'}, dimensions={3} | all-to-all | bytes 2097152 | tf_op jit(solution)/shard_map/all_to_all | solution.py:163
  (167 shorter events, 331.9 us)
Async XLA Ops:
  0.6 6.8 copy-start
  1.6 7.0 copy-start.8
  2.6 6.0 copy-start.10
  21.7 55.9 %all-to-all-start = ((f32[6,2,1,128,512]{4,1,0,2,3:T(2,128)}), f32[6,2,1,128,512]{4,1,0,2,3:T(2,128)}, u32[]{:S(2)}, u32[]{:S(2)}) async-start(f32[6,2,1,128,512]{4,1,0,2,3:T(2,128)} %copy.88), calls=%async_computation | async-start | bytes 6291456 | tf_op jit(solution)/shard_map/all_to_all | solution.py:155
  31.7 61.7 %copy-start.12 = (f32[1,16,16,1,256]{4,2,1,0,3:T(8,128)}, f32[1,16,16,1,256]{4,2,1,0,3:T(8,128)S(1)}, u32[]{:S(2)}) copy-start(f32[1,16,16,1,256]{4,2,1,0,3:T(8,128)S(1)} %get-tuple-element.49) | copy-start | bytes 786436
  31.7 61.7 %copy-start.15 = (f32[1,16,16,1,256]{4,2,1,0,3:T(8,128)}, f32[1,16,16,1,256]{4,2,1,0,3:T(8,128)S(1)}, u32[]{:S(2)}) copy-start(f32[1,16,16,1,256]{4,2,1,0,3:T(8,128)S(1)} %get-tuple-element.50) | copy-start | bytes 786436
  31.7 61.7 %copy-start.18 = (f32[1,16,16,1,256]{4,2,1,0,3:T(8,128)}, f32[1,16,16,1,256]{4,2,1,0,3:T(8,128)S(1)}, u32[]{:S(2)}) copy-start(f32[1,16,16,1,256]{4,2,1,0,3:T(8,128)S(1)} %get-tuple-element.51) | copy-start | bytes 786436
  138.0 44.1 %all-to-all-start.1 = ((f32[6,2,1,256,256]{4,1,0,2,3:T(2,128)}), f32[6,2,1,256,256]{4,1,0,2,3:T(2,128)}, u32[]{:S(2)}, u32[]{:S(2)}) async-start(f32[6,2,1,256,256]{4,1,0,2,3:T(2,128)} %copy.91), calls=%async_computation.1 | async-start | bytes 6291456 | tf_op jit(solution)/shard_map/all_to_all | solution.py:163
  149.0 42.4 %copy-start.21 = (f32[1,8,32,1,256]{4,2,1,0,3:T(8,128)}, f32[1,8,32,1,256]{4,2,1,0,3:T(8,128)S(1)}, u32[]{:S(2)}) copy-start(f32[1,8,32,1,256]{4,2,1,0,3:T(8,128)S(1)} %get-tuple-element.52) | copy-start | bytes 786436
  149.0 42.4 %copy-start.24 = (f32[1,8,32,1,256]{4,2,1,0,3:T(8,128)}, f32[1,8,32,1,256]{4,2,1,0,3:T(8,128)S(1)}, u32[]{:S(2)}) copy-start(f32[1,8,32,1,256]{4,2,1,0,3:T(8,128)S(1)} %get-tuple-element.53) | copy-start | bytes 786436
  149.0 42.4 %copy-start.27 = (f32[1,8,32,1,256]{4,2,1,0,3:T(8,128)}, f32[1,8,32,1,256]{4,2,1,0,3:T(8,128)S(1)}, u32[]{:S(2)}) copy-start(f32[1,8,32,1,256]{4,2,1,0,3:T(8,128)S(1)} %get-tuple-element.54) | copy-start | bytes 786436
  369.9 5.1 copy-start.9
  369.9 5.1 copy-start.11
  369.9 51.7 %all-to-all-start.3 = ((f32[6,2,16,8,512]{4,3,1,0,2:T(8,128)}), f32[6,2,16,8,512]{4,3,1,0,2:T(8,128)}, u32[]{:S(2)}, u32[]{:S(2)}) async-start(f32[6,2,16,8,512]{4,3,1,0,2:T(8,128)} %reshape.527), calls=%async_computation.3 | async-start | bytes 6291456 | tf_op jit(solution)/shard_map/all_to_all | solution.py:194
  552.8 16.0 %copy-start.13 = (f32[1,16,16,1,256]{4,2,1,0,3:T(8,128)S(1)}, f32[1,16,16,1,256]{4,2,1,0,3:T(8,128)}, u32[]{:S(2)}) copy-start(f32[1,16,16,1,256]{4,2,1,0,3:T(8,128)} %copy-done.12) | copy-start | bytes 786436
  552.8 16.0 %copy-start.16 = (f32[1,16,16,1,256]{4,2,1,0,3:T(8,128)S(1)}, f32[1,16,16,1,256]{4,2,1,0,3:T(8,128)}, u32[]{:S(2)}) copy-start(f32[1,16,16,1,256]{4,2,1,0,3:T(8,128)} %copy-done.15) | copy-start | bytes 786436
  552.8 16.0 %copy-start.19 = (f32[1,16,16,1,256]{4,2,1,0,3:T(8,128)S(1)}, f32[1,16,16,1,256]{4,2,1,0,3:T(8,128)}, u32[]{:S(2)}) copy-start(f32[1,16,16,1,256]{4,2,1,0,3:T(8,128)} %copy-done.18) | copy-start | bytes 786436
  658.2 9.5 copy-start.22
  658.2 9.5 copy-start.25
  658.2 9.5 copy-start.28
  989.7 4.9 copy-start.20
  1032.7 10.0 copy-start.6
  1032.7 10.0 copy-start.7
  1076.5 37.6 %all-to-all-start.11 = ((f32[1,2,16,8,512]{4,3,1,0,2:T(8,128)}), f32[1,2,16,8,512]{4,3,1,0,2:T(8,128)S(1)}, u32[]{:S(2)}, u32[]{:S(2)}) async-start(f32[1,2,16,8,512]{4,3,1,0,2:T(8,128)} %reshape.533), calls=%async_computation.11 | async-start | bytes 1048576 | tf_op jit(solution)/shard_map/all_to_all | solution.py:194
  (14 other events, 31.3 us)
where the time goes:
time: 1140 us; the launch traced here: 1130 us
  matrix products  389 us (34%)
  blocking collectives  300 us (26%)
  local copies, waits for them, and re-layouts  263 us (23%)
  waiting for transfers between devices  124 us (11%)
  other arithmetic  26.5 us (2%)
  starting transfers between devices  24 us (2%)
    dot_general x18, matrix products, contract(): jnp.einsum(form, data, table, precision=lax.Precision.HIGHEST, preferred_...  389 us
    all_to_all x3, blocking collectives, inverse_col(): lax.all_to_all(spectrum, ROW, split_axis=2, concat_axis=3, tiled=True)  98.5 us
    reshape x6, local copies, waits for them, and re-layouts, inverse_col(): spectrum = spectrum.reshape(members, 2, ncols, kz_local, local_x * local_y)  86.4 us
    all_to_all x2, blocking collectives, forward_col(): lax.all_to_all(spectrum, ROW, split_axis=3, concat_axis=2, tiled=True)  65.2 us
    all_to_all x2, blocking collectives, forward_col(): lax.all_to_all(spectrum, COL, split_axis=3, concat_axis=2, tiled=True)  61.6 us
    all_to_all x2, waiting for transfers between devices, inverse_col(): lax.all_to_all(spectrum, COL, split_axis=2, concat_axis=3, tiled=True)  46.6 us
    all_to_all x1, waiting for transfers between devices, forward_col(): lax.all_to_all(spectrum, COL, split_axis=3, concat_axis=2, tiled=True)  45.8 us
    all_to_all x1, blocking collectives, inverse_col(): lax.all_to_all(spectrum, COL, split_axis=2, concat_axis=3, tiled=True)  42.3 us
  transfers between devices with their start and end apart: 4, of which 3 were waited for; matrix products, arithmetic and copies ran while one was open for 1% of the time, Pallas kernels for 0%

commit v1 on v0

v1 whole, which is shorter than its diff:
```python
import math

import jax
import jax.numpy as jnp
import numpy as np
from jax import lax
from jax.experimental import pallas as pl
from jax.experimental.pallas import tpu as pltpu
from jax.sharding import PartitionSpec as P

F32 = jnp.float32
B16 = jnp.bfloat16
N = 256
H = 128
ITERS = 2
STEP = 2.0 * math.pi / N
SCALE = 1.0 / float(N) ** 3

FIRST_LOW = 1.0
FIRST_RISE = 0.6
SHEAR_LOW = 0.7
SHEAR_RISE = 0.8
FIRST_REF = 1.3
SHEAR_REF = 1.1
BETA_REF = 2.4 / 3.5
EIGEN_STRAIN = 0.5
WELL_HEIGHT = 1.0
TIME_STEP = 0.5
GRADIENT_ENERGY = 0.5

XX, YY, ZZ, YZ, XZ, XY = range(6)


def base_tables():
    index = np.arange(N)
    angle = (index[:, None] * index[None, :] % N) * (2.0 * np.pi / N)
    parts = []
    for table in (np.cos(angle), np.sin(angle)):
        lead = table.astype(np.float32).astype(jnp.bfloat16)
        rest = (table - lead.astype(np.float64)).astype(np.float32).astype(jnp.bfloat16)
        parts += [lead, rest]
    return np.stack(parts)


def split(value):
    lead = value.astype(B16)
    rest = (value - lead.astype(F32)).astype(B16)
    return lead, rest


def dot(a, b):
    return jnp.dot(a, b, preferred_element_type=F32)


def fill_left(base, out, sine_sign):
    for block, part in enumerate((0, 0, 1)):
        at = block * 2 * N
        cosine, sine = base[part], base[2 + part]
        upper, lower = (sine, -sine) if sine_sign > 0 else (-sine, sine)
        out[0:N, at : at + N] = cosine
        out[0:N, at + N : at + 2 * N] = upper
        out[N : 2 * N, at : at + N] = lower
        out[N : 2 * N, at + N : at + 2 * N] = cosine


def fill_right(base, out, sine_sign):
    for block, part in enumerate((0, 0, 1)):
        at = block * 2 * N
        cosine, sine = base[part], base[2 + part]
        upper, lower = (sine, -sine) if sine_sign > 0 else (-sine, sine)
        out[at : at + N, 0:N] = cosine
        out[at : at + N, N : 2 * N] = upper
        out[at + N : at + 2 * N, 0:N] = lower
        out[at + N : at + 2 * N, N : 2 * N] = cosine


def fill_z_ahead(base, out):
    for block, part in enumerate((0, 0, 1)):
        at = block * N
        out[0:H, at : at + N] = base[part, 0:H, :]
        out[H:N, at : at + N] = -base[2 + part, 0:H, :]


def fill_z_back(base, out):
    column = lax.broadcasted_iota(jnp.int32, (N, H), 1)
    weight = jnp.where(column == 0, 1.0, 2.0)
    for block, part in enumerate((0, 0, 1)):
        at = block * N
        out[:, at : at + H] = (base[part, :, 0:H].astype(F32) * weight).astype(B16)
        out[:, at + H : at + N] = (base[2 + part, :, 0:H].astype(F32) * -weight).astype(B16)


def put_pair(wide, x, real, imag):
    rows = pl.ds(x * H, H)
    for at, value in ((0, real), (N, imag)):
        lead, rest = split(value)
        wide[rows, at : at + N] = lead
        wide[rows, 2 * N + at : 3 * N + at] = rest
        wide[rows, 4 * N + at : 5 * N + at] = lead


def z_ahead(field, z_table, tall, wide, x):
    lead, rest = split(field)
    tall[0:N, :] = lead
    tall[N : 2 * N, :] = rest
    tall[2 * N : 3 * N, :] = lead
    spectrum = dot(z_table[...], tall[0 : 3 * N, :])
    put_pair(wide, x, spectrum[0:H], spectrum[H:N])


def z_back(real, imag, z_table, tall):
    for at, value in ((0, real), (H, imag)):
        lead, rest = split(value)
        tall[at : at + H, :] = lead
        tall[N + at : N + at + H, :] = rest
        tall[2 * N + at : 2 * N + at + H, :] = lead
    return dot(z_table[...], tall[0 : 3 * N, :])


def store_planes(out, field, spectrum):
    for x in range(2):
        for block in range(4):
            out[field, pl.ds(x * 4 + block, H, stride=8), :] = spectrum[
                x * H : (x + 1) * H, block * H : (block + 1) * H
            ]


def load_plane(landed, field, x):
    parts = [landed[field, pl.ds(x * 4 + block, H, stride=8), :] for block in range(4)]
    return jnp.concatenate(parts[0:2], axis=1), jnp.concatenate(parts[2:4], axis=1)


def x_ahead(landed, field, x_table, tall, spectrum, slot):
    for part in range(2):
        for half in range(2):
            rows = landed[field, pl.ds(part * 2 + half, N, stride=4), :]
            lead, rest = split(rows)
            at, lanes = part * N, slice(half * H, (half + 1) * H)
            tall[at : at + N, lanes] = lead
            tall[2 * N + at : 3 * N + at, lanes] = rest
            tall[4 * N + at : 5 * N + at, lanes] = lead
    spectrum[slot] = dot(x_table[...], tall[...])


def x_back(spectrum, slot, x_table, tall, out, field):
    lead, rest = split(spectrum[slot])
    tall[0 : 2 * N, :] = lead
    tall[2 * N : 4 * N, :] = rest
    tall[4 * N : 6 * N, :] = lead
    lines = dot(x_table[...], tall[...])
    for part in range(2):
        for half in range(2):
            out[field, pl.ds(part * 2 + half, N, stride=4), :] = lines[
                part * N : (part + 1) * N, half * H : (half + 1) * H
            ]


def signed(index):
    return jnp.where(index < H, index, index - N).astype(F32) * STEP


def lane_wave(rows, lanes=N):
    return signed(lax.broadcasted_iota(jnp.int32, (rows, lanes), 1))


def row_wave_z():
    return lax.broadcasted_iota(jnp.int32, (H, N), 0).astype(F32) * STEP


CHUNK = 32


def chunk_waves(chunk, kz):
    row = chunk * CHUNK + lax.broadcasted_iota(jnp.int32, (CHUNK, N), 0)
    wave_x = signed(row)
    wave_y = lane_wave(CHUNK)
    wave_z = kz.astype(F32) * STEP
    square = wave_x * wave_x + wave_y * wave_y + wave_z * wave_z
    return wave_x, wave_y, wave_z, square


def green_first(spectrum, source, kz):
    def body(chunk, _):
        wave_x, wave_y, wave_z, square = chunk_waves(chunk, kz)
        nonzero = square > 0.0
        safe = jnp.where(nonzero, square, 1.0)
        factor = jnp.where(nonzero, (BETA_REF - 1.0) * SCALE / (SHEAR_REF * safe), 0.0)
        for part in range(2):
            rows = pl.ds(part * N + chunk * CHUNK, CHUNK)
            psi = spectrum[source, rows, :] * factor
            once = wave_x * psi
            spectrum[0, rows, :] = wave_x * once
            spectrum[1, rows, :] = once
            spectrum[2, rows, :] = psi
        return 0

    lax.fori_loop(0, N // CHUNK, body, 0)


def green_full(spectrum, kz):
    def body(chunk, _):
        wave_x, wave_y, wave_z, square = chunk_waves(chunk, kz)
        nonzero = square > 0.0
        safe = jnp.where(nonzero, square, 1.0)
        scale = jnp.where(nonzero, -SCALE / (SHEAR_REF * safe), 0.0)
        ratio = BETA_REF / safe
        for part in range(2):
            rows = pl.ds(part * N + chunk * CHUNK, CHUNK)
            first, second, third = (spectrum[slot, rows, :] for slot in range(3))
            force_x = wave_x * first + wave_y * second + wave_z * third
            force_y = wave_x * second + spectrum[3, rows, :]
            force_z = wave_x * third + spectrum[4, rows, :]
            along = (wave_x * force_x + wave_y * force_y + wave_z * force_z) * ratio
            moved_x = scale * (force_x - along * wave_x)
            moved_y = scale * (force_y - along * wave_y)
            moved_z = scale * (force_z - along * wave_z)
            spectrum[0, rows, :] = wave_x * moved_x
            spectrum[1, rows, :] = moved_y
            spectrum[2, rows, :] = moved_z
            spectrum[3, rows, :] = 0.5 * (wave_x * moved_z + wave_z * moved_x)
            spectrum[4, rows, :] = 0.5 * (wave_x * moved_y + wave_y * moved_x)
        return 0

    lax.fori_loop(0, N // CHUNK, body, 0)


def relax(spectrum, drive, conc, kz):
    def body(chunk, _):
        _, _, _, square = chunk_waves(chunk, kz)
        inverse = SCALE / (1.0 + TIME_STEP * GRADIENT_ENERGY * square * square)
        for part in range(2):
            rows = pl.ds(part * N + chunk * CHUNK, CHUNK)
            value = conc[rows, :] - TIME_STEP * square * spectrum[drive, rows, :]
            spectrum[drive, rows, :] = value * inverse
        return 0

    lax.fori_loop(0, N // CHUNK, body, 0)


ROWS = 32


def eigen_stress(conc):
    rise = (3.0 * FIRST_RISE + 2.0 * SHEAR_RISE) * EIGEN_STRAIN
    low = (3.0 * FIRST_LOW + 2.0 * SHEAR_LOW) * EIGEN_STRAIN
    return (0.5 - conc) * (rise * (conc + 0.5) + low)


def polarize(parts, conc):
    first = FIRST_LOW + FIRST_RISE * conc
    excess = 2.0 * (SHEAR_LOW + SHEAR_RISE * conc - SHEAR_REF)
    normal = (first - FIRST_REF) * (parts[0] + parts[1] + parts[2]) + eigen_stress(conc)
    return [normal + excess * p for p in parts[:3]] + [excess * p for p in parts[3:]]


def potential(parts, conc):
    first = FIRST_LOW + FIRST_RISE * conc
    shear = SHEAR_LOW + SHEAR_RISE * conc
    dilation = EIGEN_STRAIN * conc
    d = [p - dilation for p in parts[:3]]
    trace = d[0] + d[1] + d[2]
    energy = d[0] * d[0] + d[1] * d[1] + d[2] * d[2]
    energy = energy + 2.0 * (parts[3] * parts[3] + parts[4] * parts[4] + parts[5] * parts[5])
    chemical = 2.0 * WELL_HEIGHT * conc * (1.0 - conc) * (1.0 - 2.0 * conc)
    return (
        chemical
        + 0.5 * FIRST_RISE * trace * trace
        + SHEAR_RISE * energy
        - EIGEN_STRAIN * (3.0 * first + 2.0 * shear) * trace
    )


def ahead_first(plain, conc, eigen):
    for x in range(2):
        conc[x] = plain[x].T

        def body(chunk, _):
            rows = pl.ds(chunk * ROWS, ROWS)
            eigen[x, rows, :] = eigen_stress(conc[x, rows, :])
            return 0

        lax.fori_loop(0, N // ROWS, body, 0)


def field_ahead(field_of, z_table, y_table, tall, wide):
    for x in range(2):
        z_ahead(field_of(x), z_table, tall, wide, x)
    return dot(wide[...], y_table[...])


def field_back(parts_of, factor, y_table, z_table, tall, wide, out):
    for x in range(2):
        put_pair(wide, x, *parts_of(x))
    lines = dot(wide[...], y_table[...])
    for x in range(2):
        real, imag = lines[x * H : (x + 1) * H, 0:N], lines[x * H : (x + 1) * H, N : 2 * N]
        if factor is not None:
            real, imag = factor * real, factor * imag
        out(x, z_back(real, imag, z_table, tall))


def strain_first(landed, y_back, z_back_table, tall, wide, strain):
    wave_y, wave_z = lane_wave(H), row_wave_z()

    def scaled(field, power):
        def parts_of(x):
            real, imag = load_plane(landed, field, x)
            for _ in range(power):
                real, imag = wave_y * real, wave_y * imag
            return real, imag

        return parts_of

    for target, field, power, factor in (
        (XX, 0, 0, None),
        (XY, 1, 1, None),
        (XZ, 1, 0, wave_z),
        (YY, 2, 2, None),
        (YZ, 2, 1, wave_z),
        (ZZ, 2, 0, wave_z * wave_z),
    ):

        def put(x, value, target=target):
            strain[target, x] = value

        field_back(scaled(field, power), factor, y_back, z_back_table, tall, wide, put)


def strain_full(landed, y_back, z_back_table, tall, wide, strain):
    wave_y, wave_z = lane_wave(H), row_wave_z()

    def plain(field):
        return lambda x: load_plane(landed, field, x)

    def along_y(x):
        real, imag = load_plane(landed, 1, x)
        return wave_y * real, wave_y * imag

    def shear(x):
        real_y, imag_y = load_plane(landed, 1, x)
        real_z, imag_z = load_plane(landed, 2, x)
        return (
            0.5 * (wave_y * real_z + wave_z * real_y),
            0.5 * (wave_y * imag_z + wave_z * imag_y),
        )

    for target, parts_of, factor in (
        (XX, plain(0), None),
        (XZ, plain(3), None),
        (XY, plain(4), None),
        (YY, along_y, None),
        (YZ, shear, None),
        (ZZ, plain(2), wave_z),
    ):

        def put(x, value, target=target):
            strain[target, x] = value

        field_back(parts_of, factor, y_back, z_back_table, tall, wide, put)


def sum_squares(parts):
    total = parts[0] * parts[0]
    for part in parts[1:]:
        total = total + part * part
    return total


def k1(base, plain, conc, out, eigen, tall, wide, z_table, y_table):
    fill_z_ahead(base, z_table)
    fill_right(base, y_table, -1)
    ahead_first(plain, conc, eigen)
    store_planes(out, 0, field_ahead(lambda x: eigen[x], z_table, y_table, tall, wide))
    store_planes(out, 1, field_ahead(lambda x: conc[x], z_table, y_table, tall, wide))


def plane_z():
    return lax.axis_index("row") * 16 + lax.axis_index("col")


def k2(base, landed, out, conc, spectrum, tall, ahead, back):
    fill_left(base, ahead, 1)
    fill_left(base, back, -1)
    x_ahead(landed, 0, ahead, tall, spectrum, 3)
    green_first(spectrum, 3, plane_z())
    for slot in range(3):
        x_back(spectrum, slot, back, tall, out, slot)
    x_ahead(landed, 1, ahead, tall, spectrum, 3)
    conc[...] = spectrum[3]


def k3(base, landed, conc, out, strain, partial, work, planes, tall, wide, zf, zb, yf, yb):
    fill_z_ahead(base, zf)
    fill_z_back(base, zb)
    fill_right(base, yf, -1)
    fill_right(base, yb, 1)
    strain_first(landed, yb, zb, tall, wide, strain)
    partial[...] = jnp.zeros_like(partial)
    for x in range(2):

        def body(chunk, _):
            rows = pl.ds(chunk * ROWS, ROWS)
            parts = [strain[i, x, rows, :] for i in range(6)]
            partial[...] += sum_squares(parts)
            for i, value in enumerate(polarize(parts, conc[x, rows, :])):
                work[i, x, rows, :] = value
            return 0

        lax.fori_loop(0, N // ROWS, body, 0)
    stress_ahead(work, out, planes, tall, wide, zf, yf)


def stress_ahead(work, out, planes, tall, wide, zf, yf):
    wave_y = lane_wave(H)
    wave_y = jnp.concatenate([wave_y, wave_y], axis=1)
    wave_y = jnp.concatenate([wave_y, wave_y], axis=0)
    row = lax.broadcasted_iota(jnp.int32, (N, 2 * N), 0)
    wave_z = jnp.where(row < H, row, row - H).astype(F32) * STEP

    def spectrum_of(component):
        return field_ahead(lambda x: work[component, x], zf, yf, tall, wide)

    store_planes(out, 0, spectrum_of(XX))
    store_planes(out, 1, spectrum_of(XY))
    store_planes(out, 2, spectrum_of(XZ))
    planes[...] = spectrum_of(YZ)
    store_planes(out, 3, wave_y * spectrum_of(YY) + wave_z * planes[...])
    store_planes(out, 4, wave_z * spectrum_of(ZZ) + wave_y * planes[...])


def k4(base, landed, out, spectrum, tall, ahead, back):
    fill_left(base, ahead, 1)
    fill_left(base, back, -1)

    def go(slot, _):
        x_ahead(landed, slot, ahead, tall, spectrum, slot)
        return 0

    lax.fori_loop(0, 5, go, 0)
    green_full(spectrum, plane_z())

    def come(slot, _):
        x_back(spectrum, slot, back, tall, out, slot)
        return 0

    lax.fori_loop(0, 5, come, 0)


def k5(base, landed, conc, before, out, strain, partial, work, drive, tall, wide, zf, zb, yf, yb):
    fill_z_ahead(base, zf)
    fill_z_back(base, zb)
    fill_right(base, yf, -1)
    fill_right(base, yb, 1)
    strain_full(landed, yb, zb, tall, wide, work)
    partial[...] = jnp.zeros_like(partial)
    for x in range(2):

        def body(chunk, _):
            rows = pl.ds(chunk * ROWS, ROWS)
            parts = [work[i, x, rows, :] for i in range(6)]
            partial[...] += sum_squares([p - before[i, x, rows, :] for i, p in enumerate(parts)])
            drive[x, rows, :] = potential(parts, conc[x, rows, :])
            return 0

        lax.fori_loop(0, N // ROWS, body, 0)
    store_planes(out, 0, field_ahead(lambda x: drive[x], zf, yf, tall, wide))

    def turn(i, _):
        for x in range(2):
            strain[i, x] = work[i, x].T
        return 0

    lax.fori_loop(0, 6, turn, 0)


def k6(base, landed, conc, out, spectrum, tall, ahead, back):
    fill_left(base, ahead, 1)
    fill_left(base, back, -1)
    x_ahead(landed, 0, ahead, tall, spectrum, 0)
    relax(spectrum, 0, conc, plane_z())
    x_back(spectrum, 0, back, tall, out, 0)


def k7(base, landed, plain, tall, wide, zb, yb):
    fill_z_back(base, zb)
    fill_right(base, yb, 1)

    def put(x, value):
        plain[x] = value.T

    field_back(lambda x: load_plane(landed, 0, x), None, yb, zb, tall, wide, put)


TALL = pltpu.VMEM((6 * N, N), B16)
WIDE = pltpu.VMEM((2 * H, 6 * N), B16)
ZTAB = pltpu.VMEM((N, 3 * N), B16)
RIGHT = pltpu.VMEM((6 * N, 2 * N), B16)
LEFT = pltpu.VMEM((2 * N, 6 * N), B16)


def planes_of(n):
    return pltpu.VMEM((n, 2, N, N), F32)


def shape(*dims):
    return jax.ShapeDtypeStruct(dims, F32)


def call(body, outs, scratch, *args):
    vmem = pl.BlockSpec(memory_space=pltpu.VMEM)
    return pl.pallas_call(
        body,
        out_shape=outs,
        in_specs=[vmem] * len(args),
        out_specs=jax.tree.map(lambda _: vmem, outs),
        scratch_shapes=scratch,
        compiler_params=pltpu.CompilerParams(vmem_limit_bytes=60 * 2**20),
        name=body.__name__,
    )(*args)


ALL = ("row", "col")


def exchange(data):
    fields = data.shape[0]
    data = data.reshape(fields, H, 8, H)
    data = lax.all_to_all(data, ALL, split_axis=1, concat_axis=1, tiled=True)
    return data.reshape(fields, 8 * H, H)


def shards(base, concentration):
    plain = lax.all_to_all(concentration, "col", split_axis=0, concat_axis=1, tiled=True)
    conc, data = call(
        k1, [shape(2, N, N), shape(2, 8 * H, H)], [pltpu.VMEM((2, N, N), F32), TALL, WIDE, ZTAB, RIGHT], base, plain
    )
    data, conc_hat = call(
        k2,
        [shape(3, 8 * H, H), shape(2 * N, N)],
        [pltpu.VMEM((4, 2 * N, N), F32), TALL, LEFT, LEFT],
        base,
        exchange(data),
    )
    data, before, first = call(
        k3,
        [shape(5, 8 * H, H), shape(6, 2, N, N), shape(ROWS, N)],
        [planes_of(6), pltpu.VMEM((N, 2 * N), F32), TALL, WIDE, ZTAB, ZTAB, RIGHT, RIGHT],
        base,
        exchange(data),
        conc,
    )
    (data,) = call(
        k4,
        [shape(5, 8 * H, H)],
        [pltpu.VMEM((5, 2 * N, N), F32), TALL, LEFT, LEFT],
        base,
        exchange(data),
    )
    data, strain, second = call(
        k5,
        [shape(1, 8 * H, H), shape(6, 2, N, N), shape(ROWS, N)],
        [planes_of(6), pltpu.VMEM((2, N, N), F32), TALL, WIDE, ZTAB, ZTAB, RIGHT, RIGHT],
        base,
        exchange(data),
        conc,
        before,
    )
    sums = lax.psum(jnp.stack([jnp.sum(first), jnp.sum(second)]), ALL)
    strain = lax.all_to_all(strain, "col", split_axis=2, concat_axis=1, tiled=True)
    (data,) = call(
        k6,
        [shape(1, 8 * H, H)],
        [pltpu.VMEM((1, 2 * N, N), F32), TALL, LEFT, LEFT],
        base,
        exchange(data),
        conc_hat,
    )
    (plain,) = call(k7, [shape(2, N, N)], [TALL, WIDE, ZTAB, RIGHT], base, exchange(data))
    result = lax.all_to_all(plain, "col", split_axis=1, concat_axis=0, tiled=True)
    return result, strain, jnp.sqrt(sums * SCALE)


def solution(mesh):
    base = base_tables()
    body = jax.shard_map(
        shards,
        mesh=mesh,
        in_specs=(P(), P("row", "col", None)),
        out_specs=(P("row", "col", None), P(None, "row", "col", None), P()),
        check_vma=False,
    )

    def run(concentration):
        return body(jnp.asarray(base), concentration)

    return run
```

time: 1140 us -> 385 us (0.34)
  matrix products: 389 us -> 0 us
  local copies, waits for them, and re-layouts: 263 us -> 23.6 us
  waiting for transfers between devices: 124 us -> 6.69 us
  Pallas kernels: 0 us -> 54.1 us
  other arithmetic: 26.5 us -> 3.1 us
  starting transfers between devices: 24 us -> 7.99 us
  blocking collectives: 300 us -> 288 us
    dot_general x18 -> x0, matrix products: 389 us -> none  [contract(): jnp.einsum(form, data, table, precision=lax.Precision.HIGHEST, preferred_...]
    reshape x25 -> x4, local copies, waits for them, and re-layouts: 236 us -> 6.62 us  [exchange(): data = data.reshape(fields, H, 8, H)]
    all_to_all x4 -> x2, waiting for transfers between devices: 124 us -> 6.69 us  [the longest x1 6.69 us: shards(): lax.all_to_all(plain, 'col', split_axis=1, concat_axis=0, tiled=True)]
    all_to_all x8 -> x7, blocking collectives: 268 us -> 191 us  [the longest x6 172 us: exchange(): data = lax.all_to_all(data, ALL, split_axis=1, concat_axis=1, tiled=True)]
    psum x4 -> x1, blocking collectives: 32.1 us -> 96.2 us  [shards(): sums = lax.psum(jnp.stack([jnp.sum(first), jnp.sum(second)]), ALL)]
    pallas_call x0 -> x7, Pallas kernels: none -> 54.1 us  [call(): pl.pallas_call(body, out_shape=outs, in_specs=[vmem] * len(args), out_spe...]
    all_to_all x4 -> x2, starting transfers between devices: 24 us -> 7.99 us  [the longest x1 4.25 us: shards(): lax.all_to_all(plain, 'col', split_axis=1, concat_axis=0, tiled=True)]
    unnamed x20 -> x0, other arithmetic: 12.3 us -> none
  transfers between devices with their start and end apart: 4 -> 2, of which waited for: 3 -> 1; matrix products, arithmetic and copies ran while one was open for 1% -> 2% of each run, Pallas kernels for 0% -> 0%
where the time goes in v1:
time: 385 us; the launch traced here: 384 us
  blocking collectives  288 us (75%)
  Pallas kernels  54.1 us (14%)
  local copies, waits for them, and re-layouts  23.6 us (6%)
  starting transfers between devices  7.99 us (2%)
  waiting for transfers between devices  6.69 us (2%)
    all_to_all x6, blocking collectives, exchange(): data = lax.all_to_all(data, ALL, split_axis=1, concat_axis=1, tiled=True)  172 us
    psum x1, blocking collectives, shards(): sums = lax.psum(jnp.stack([jnp.sum(first), jnp.sum(second)]), ALL)  96.2 us
    pallas_call x7, Pallas kernels, call(): pl.pallas_call(body, out_shape=outs, in_specs=[vmem] * len(args), out_spe...  54.1 us
    all_to_all x1, blocking collectives, shards(): lax.all_to_all(concentration, 'col', split_axis=0, concat_axis=1, tiled=T...  19 us
  transfers between devices with their start and end apart: 2, of which 1 were waited for; matrix products, arithmetic and copies ran while one was open for 2% of the time, Pallas kernels for 0%

profile of v1, /device:TPU:1, one launch (start us, length us, event | category | flops | bytes accessed | tf_op | source)
XLA Modules:
  0.0 383.7 jit_solution(17798528635937724536)
XLA Ops:
  0.6 19.0 %all_to_all.84 = f32[32,16,256]{2,1,0:T(8,128)S(1)} all-to-all(f32[32,16,256]{2,1,0:T(8,128)} %param.2), channel_id=1, replica_groups=mesh['row'=8,'col'=16] {'col'}, dimensions={0} | all-to-all | bytes 1048576 | tf_op jit(solution)/shard_map/all_to_all | solution.py:533
  20.5 4.3 %k1.1 = (f32[2,256,256]{2,1,0:T(8,128)}, f32[2,1024,128]{2,1,0:T(8,128)}) custom-call(bf16[4,256,256]{2,1,0:T(8,128)(2,1)} %constant.6.clone.base, f32[2,256,256]{2,1,0:T(8,128)} %bitcast.47), custom_call_target="tpu_custom_call" | custom-call | tf_op jit(solution)/shard_map/k1/pallas_call | solution.py:511
  26.1 25.9 %all_to_all.85 = f32[2,128,8,128]{3,2,0,1:T(8,128)S(1)} all-to-all(f32[2,128,8,128]{3,2,0,1:T(8,128)S(1)} %copy.9), channel_id=1, replica_groups=mesh['row'=8,'col'=16] {'row','col'}, dimensions={1} | all-to-all | bytes 2097152 | tf_op jit(solution)/shard_map/all_to_all | solution.py:528
  53.0 5.6 %k2.1 = (f32[3,1024,128]{2,1,0:T(8,128)}, f32[512,256]{1,0:T(8,128)}) custom-call(bf16[4,256,256]{2,1,0:T(8,128)(2,1)} %constant.6.clone.base, f32[2,1024,128]{2,1,0:T(8,128)} %bitcast.43), custom_call_target="tpu_custom_call" | custom-call | tf_op jit(solution)/shard_map/k2/pallas_call | solution.py:511
  60.1 28.1 %all_to_all.86 = f32[3,128,8,128]{3,2,0,1:T(8,128)S(1)} all-to-all(f32[3,128,8,128]{3,2,0,1:T(8,128)S(1)} %copy.11), channel_id=1, replica_groups=mesh['row'=8,'col'=16] {'row','col'}, dimensions={1} | all-to-all | bytes 3145728 | tf_op jit(solution)/shard_map/all_to_all | solution.py:528
  89.5 13.3 %k3.1 = (f32[5,1024,128]{2,1,0:T(8,128)}, f32[6,2,256,256]{3,2,1,0:T(8,128)}, f32[32,256]{1,0:T(8,128)}) custom-call(bf16[4,256,256]{2,1,0:T(8,128)(2,1)} %constant.6.clone.base, f32[3,1024,128]{2,1,0:T(8,128)} %bitcast.42, f32[2,256,256]{2,1,0:T(8,128)} %get-tuple-element.15.conc), custom_call_target="tpu_custom_call" | custom-call | tf_op jit(solution)/shard_map/k3/pallas_call | solution.py:511
  102.7 1.9 copy.13
  104.6 39.1 %all_to_all.87 = f32[5,128,8,128]{3,2,0,1:T(8,128)S(1)} all-to-all(f32[5,128,8,128]{3,2,0,1:T(8,128)S(1)} %copy.13), channel_id=1, replica_groups=mesh['row'=8,'col'=16] {'row','col'}, dimensions={1} | all-to-all | bytes 5242880 | tf_op jit(solution)/shard_map/all_to_all | solution.py:528
  145.4 10.6 %k4.1 = f32[5,1024,128]{2,1,0:T(8,128)} custom-call(bf16[4,256,256]{2,1,0:T(8,128)(2,1)} %constant.6.clone.base, f32[5,1024,128]{2,1,0:T(8,128)} %bitcast.40), custom_call_target="tpu_custom_call" | custom-call | tf_op jit(solution)/shard_map/k4/pallas_call | solution.py:511
  156.1 1.9 copy.15
  158.0 39.8 %all_to_all.88 = f32[5,128,8,128]{3,2,0,1:T(8,128)S(1)} all-to-all(f32[5,128,8,128]{3,2,0,1:T(8,128)S(1)} %copy.15), channel_id=1, replica_groups=mesh['row'=8,'col'=16] {'row','col'}, dimensions={1} | all-to-all | bytes 5242880 | tf_op jit(solution)/shard_map/all_to_all | solution.py:528
  199.5 12.8 %k5.1 = (f32[1,1024,128]{2,1,0:T(8,128)}, f32[6,2,256,256]{3,2,1,0:T(8,128)}, f32[32,256]{1,0:T(8,128)}) custom-call(bf16[4,256,256]{2,1,0:T(8,128)(2,1)} %constant.6.clone.base, f32[5,1024,128]{2,1,0:T(8,128)} %bitcast.39, f32[2,256,256]{2,1,0:T(8,128)} %get-tuple-element.15.conc, f32[6,2,256,256]{3,2,1,0:T(8,128)} %get-tuple-element.17.before), custom_call_target="tpu_custom_call" | custom-call | tf_op jit(solution)/shard_map/k5/pallas_call | solution.py:511
  212.3 20.0 %all_to_all.89 = f32[1,128,8,128]{3,2,0,1:T(8,128)} all-to-all(f32[1,128,8,128]{3,2,0,1:T(8,128)} %bitcast.54), channel_id=1, replica_groups=mesh['row'=8,'col'=16] {'row','col'}, dimensions={1} | all-to-all | bytes 1048576 | tf_op jit(solution)/shard_map/all_to_all | solution.py:528
  232.3 4.5 %k6.1 = f32[1,1024,128]{2,1,0:T(8,128)} custom-call(bf16[4,256,256]{2,1,0:T(8,128)(2,1)} %constant.6.clone.base, f32[1,1024,128]{2,1,0:T(8,128)} %bitcast.49, f32[512,256]{1,0:T(8,128)} %get-tuple-element.19.conc), custom_call_target="tpu_custom_call" | custom-call | tf_op jit(solution)/shard_map/k6/pallas_call | solution.py:511
  236.8 19.4 %all_to_all.90 = f32[1,128,8,128]{3,2,0,1:T(8,128)} all-to-all(f32[1,128,8,128]{3,2,0,1:T(8,128)} %bitcast.50), channel_id=1, replica_groups=mesh['row'=8,'col'=16] {'row','col'}, dimensions={1} | all-to-all | bytes 1048576 | tf_op jit(solution)/shard_map/all_to_all | solution.py:528
  256.2 3.0 k7.1
  259.3 2.2 copy.19
  261.5 4.2 %all-to-all-start.7 = ((f32[2,256,256]{2,0,1:T(2,128)}), f32[2,256,256]{2,0,1:T(2,128)}, u32[]{:S(2)}, u32[]{:S(2)}) async-start(f32[2,256,256]{2,0,1:T(2,128)} %copy.19), calls=%async_computation.7 | async-start | bytes 1048576 | tf_op jit(solution)/shard_map/all_to_all | solution.py:579
  265.8 4.1 %copy.21 = f32[6,2,256,256]{3,1,0,2:T(2,128)} copy(f32[6,2,256,256]{3,2,1,0:T(8,128)S(1)} %copy-done) | data formatting | bytes 6291456 | tf_op jit(solution)/shard_map/k5/pallas_call | solution.py:511
  269.9 6.7 %all-to-all-done.7 = f32[2,256,256]{2,0,1:T(2,128)} async-done(((f32[2,256,256]{2,0,1:T(2,128)}), f32[2,256,256]{2,0,1:T(2,128)}, u32[]{:S(2)}, u32[]{:S(2)}) %all-to-all-start.7) | async-done | bytes 524320 | tf_op jit(solution)/shard_map/all_to_all | solution.py:579
  276.6 3.7 all-to-all-start.8
  282.9 96.2 %psum.7 = f32[2]{0:T(128)S(1)} all-reduce(f32[2]{0:T(128)S(1)} %pad_maximum_fusion), channel_id=1, replica_groups=mesh['row'=8,'col'=16] {'row','col'}, use_global_device_ids=true, to_apply=%region_2.0 | all-reduce | flops 2 | bytes 16 | tf_op jit(solution)/shard_map/psum | solution.py:568
  379.6 1.9 copy.20
  381.5 2.2 copy.22
  (18 shorter events, 12.4 us)
Async XLA Ops:
  236.8 29.0 %copy-start = (f32[6,2,256,256]{3,2,1,0:T(8,128)S(1)}, f32[6,2,256,256]{3,2,1,0:T(8,128)}, u32[]{:S(2)}) copy-start(f32[6,2,256,256]{3,2,1,0:T(8,128)} %get-tuple-element.20) | copy-start | bytes 9437188
  261.5 15.0 %all-to-all-start.7 = ((f32[2,256,256]{2,0,1:T(2,128)}), f32[2,256,256]{2,0,1:T(2,128)}, u32[]{:S(2)}, u32[]{:S(2)}) async-start(f32[2,256,256]{2,0,1:T(2,128)} %copy.19), calls=%async_computation.7 | async-start | bytes 1048576 | tf_op jit(solution)/shard_map/all_to_all | solution.py:579
  269.9 10.4 %copy-start.1 = (f32[32,256]{1,0:T(8,128)S(1)}, f32[32,256]{1,0:T(8,128)}, u32[]{:S(2)}) copy-start(f32[32,256]{1,0:T(8,128)} %get-tuple-element.21) | copy-start | bytes 98308
  269.9 11.1 %copy-start.2 = (f32[32,256]{1,0:T(8,128)S(1)}, f32[32,256]{1,0:T(8,128)}, u32[]{:S(2)}) copy-start(f32[32,256]{1,0:T(8,128)} %get-tuple-element.22) | copy-start | bytes 98308
  276.6 104.9 %all-to-all-start.8 = ((f32[6,2,256,256]{3,1,0,2:T(2,128)}), f32[6,2,256,256]{3,1,0,2:T(2,128)S(1)}, u32[]{:S(2)}, u32[]{:S(2)}) async-start(f32[6,2,256,256]{3,1,0,2:T(2,128)} %copy.21), calls=%async_computation.8 | async-start | bytes 6291456 | tf_op jit(solution)/shard_map/all_to_all | solution.py:569

commit v2 on v1

v2 whole, which is shorter than its diff:
```python
import math

import jax
import jax.numpy as jnp
import numpy as np
from jax import lax
from jax.experimental import pallas as pl
from jax.experimental.pallas import tpu as pltpu
from jax.sharding import PartitionSpec as P

F32 = jnp.float32
B16 = jnp.bfloat16
N = 256
H = 128
ITERS = 2
STEP = 2.0 * math.pi / N
SCALE = 1.0 / float(N) ** 3

FIRST_LOW = 1.0
FIRST_RISE = 0.6
SHEAR_LOW = 0.7
SHEAR_RISE = 0.8
FIRST_REF = 1.3
SHEAR_REF = 1.1
BETA_REF = 2.4 / 3.5
EIGEN_STRAIN = 0.5
WELL_HEIGHT = 1.0
TIME_STEP = 0.5
GRADIENT_ENERGY = 0.5

XX, YY, ZZ, YZ, XZ, XY = range(6)


def base_tables():
    index = np.arange(N)
    angle = (index[:, None] * index[None, :] % N) * (2.0 * np.pi / N)
    parts = []
    for table in (np.cos(angle), np.sin(angle)):
        lead = table.astype(np.float32).astype(jnp.bfloat16)
        rest = (table - lead.astype(np.float64)).astype(np.float32).astype(jnp.bfloat16)
        parts += [lead, rest]
    return np.stack(parts)


def split(value):
    lead = value.astype(B16)
    rest = (value - lead.astype(F32)).astype(B16)
    return lead, rest


def dot(a, b):
    return jnp.dot(a, b, preferred_element_type=F32)


def fill_left(base, out, sine_sign):
    for block, part in enumerate((0, 0, 1)):
        at = block * 2 * N
        cosine, sine = base[part], base[2 + part]
        upper, lower = (sine, -sine) if sine_sign > 0 else (-sine, sine)
        out[0:N, at : at + N] = cosine
        out[0:N, at + N : at + 2 * N] = upper
        out[N : 2 * N, at : at + N] = lower
        out[N : 2 * N, at + N : at + 2 * N] = cosine


def fill_right(base, out, sine_sign):
    for block, part in enumerate((0, 0, 1)):
        at = block * 2 * N
        cosine, sine = base[part], base[2 + part]
        upper, lower = (sine, -sine) if sine_sign > 0 else (-sine, sine)
        out[at : at + N, 0:N] = cosine
        out[at : at + N, N : 2 * N] = upper
        out[at + N : at + 2 * N, 0:N] = lower
        out[at + N : at + 2 * N, N : 2 * N] = cosine


def fill_z_ahead(base, out):
    for block, part in enumerate((0, 0, 1)):
        at = block * N
        out[0:H, at : at + N] = base[part, 0:H, :]
        out[H:N, at : at + N] = -base[2 + part, 0:H, :]


def fill_z_back(base, out):
    column = lax.broadcasted_iota(jnp.int32, (N, H), 1)
    weight = jnp.where(column == 0, 1.0, 2.0)
    for block, part in enumerate((0, 0, 1)):
        at = block * N
        out[:, at : at + H] = (base[part, :, 0:H].astype(F32) * weight).astype(B16)
        out[:, at + H : at + N] = (base[2 + part, :, 0:H].astype(F32) * -weight).astype(B16)


def put_pair(wide, x, real, imag):
    rows = pl.ds(x * H, H)
    for at, value in ((0, real), (N, imag)):
        lead, rest = split(value)
        wide[rows, at : at + N] = lead
        wide[rows, 2 * N + at : 3 * N + at] = rest
        wide[rows, 4 * N + at : 5 * N + at] = lead


def z_ahead(field, z_table, tall, wide, x):
    lead, rest = split(field)
    tall[0:N, :] = lead
    tall[N : 2 * N, :] = rest
    tall[2 * N : 3 * N, :] = lead
    spectrum = dot(z_table[...], tall[0 : 3 * N, :])
    put_pair(wide, x, spectrum[0:H], spectrum[H:N])


def z_back(real, imag, z_table, tall):
    for at, value in ((0, real), (H, imag)):
        lead, rest = split(value)
        tall[at : at + H, :] = lead
        tall[N + at : N + at + H, :] = rest
        tall[2 * N + at : 2 * N + at + H, :] = lead
    return dot(z_table[...], tall[0 : 3 * N, :])


def store_planes(out, field, spectrum):
    for x in range(2):
        for block in range(4):
            out[field, pl.ds(x * 4 + block, H, stride=8), :] = spectrum[
                x * H : (x + 1) * H, block * H : (block + 1) * H
            ]


def load_plane(landed, field, x):
    parts = [landed[field, pl.ds(x * 4 + block, H, stride=8), :] for block in range(4)]
    return jnp.concatenate(parts[0:2], axis=1), jnp.concatenate(parts[2:4], axis=1)


def x_ahead(landed, field, x_table, tall, spectrum, slot):
    for part in range(2):
        for half in range(2):
            rows = landed[field, pl.ds(part * 2 + half, N, stride=4), :]
            lead, rest = split(rows)
            at, lanes = part * N, slice(half * H, (half + 1) * H)
            tall[at : at + N, lanes] = lead
            tall[2 * N + at : 3 * N + at, lanes] = rest
            tall[4 * N + at : 5 * N + at, lanes] = lead
    spectrum[slot] = dot(x_table[...], tall[...])


def x_back(spectrum, slot, x_table, tall, out, field):
    lead, rest = split(spectrum[slot])
    tall[0 : 2 * N, :] = lead
    tall[2 * N : 4 * N, :] = rest
    tall[4 * N : 6 * N, :] = lead
    lines = dot(x_table[...], tall[...])
    for part in range(2):
        for half in range(2):
            out[field, pl.ds(part * 2 + half, N, stride=4), :] = lines[
                part * N : (part + 1) * N, half * H : (half + 1) * H
            ]


def signed(index):
    return jnp.where(index < H, index, index - N).astype(F32) * STEP


def lane_wave(rows, lanes=N):
    return signed(lax.broadcasted_iota(jnp.int32, (rows, lanes), 1))


def row_wave_z():
    return lax.broadcasted_iota(jnp.int32, (H, N), 0).astype(F32) * STEP


CHUNK = 32


def chunk_waves(chunk, kz):
    row = chunk * CHUNK + lax.broadcasted_iota(jnp.int32, (CHUNK, N), 0)
    wave_x = signed(row)
    wave_y = lane_wave(CHUNK)
    wave_z = kz.astype(F32) * STEP
    square = wave_x * wave_x + wave_y * wave_y + wave_z * wave_z
    return wave_x, wave_y, wave_z, square


def green_first(spectrum, source, kz):
    def body(chunk, _):
        wave_x, wave_y, wave_z, square = chunk_waves(chunk, kz)
        nonzero = square > 0.0
        safe = jnp.where(nonzero, square, 1.0)
        factor = jnp.where(nonzero, (BETA_REF - 1.0) * SCALE / (SHEAR_REF * safe), 0.0)
        for part in range(2):
            rows = pl.ds(part * N + chunk * CHUNK, CHUNK)
            psi = spectrum[source, rows, :] * factor
            once = wave_x * psi
            spectrum[0, rows, :] = wave_x * once
            spectrum[1, rows, :] = once
            spectrum[2, rows, :] = psi
        return 0

    lax.fori_loop(0, N // CHUNK, body, 0)


def green_full(spectrum, kz):
    def body(chunk, _):
        wave_x, wave_y, wave_z, square = chunk_waves(chunk, kz)
        nonzero = square > 0.0
        safe = jnp.where(nonzero, square, 1.0)
        scale = jnp.where(nonzero, -SCALE / (SHEAR_REF * safe), 0.0)
        ratio = BETA_REF / safe
        for part in range(2):
            rows = pl.ds(part * N + chunk * CHUNK, CHUNK)
            first, second, third = (spectrum[slot, rows, :] for slot in range(3))
            force_x = wave_x * first + wave_y * second + wave_z * third
            force_y = wave_x * second + spectrum[3, rows, :]
            force_z = wave_x * third + spectrum[4, rows, :]
            along = (wave_x * force_x + wave_y * force_y + wave_z * force_z) * ratio
            moved_x = scale * (force_x - along * wave_x)
            moved_y = scale * (force_y - along * wave_y)
            moved_z = scale * (force_z - along * wave_z)
            spectrum[0, rows, :] = wave_x * moved_x
            spectrum[1, rows, :] = 0.5 * (wave_x * moved_y + wave_y * moved_x)
            spectrum[2, rows, :] = 0.5 * (wave_x * moved_z + wave_z * moved_x)
            spectrum[3, rows, :] = moved_y
            spectrum[4, rows, :] = moved_z
        return 0

    lax.fori_loop(0, N // CHUNK, body, 0)


def relax(spectrum, drive, conc, kz):
    def body(chunk, _):
        _, _, _, square = chunk_waves(chunk, kz)
        inverse = SCALE / (1.0 + TIME_STEP * GRADIENT_ENERGY * square * square)
        for part in range(2):
            rows = pl.ds(part * N + chunk * CHUNK, CHUNK)
            value = conc[rows, :] - TIME_STEP * square * spectrum[drive, rows, :]
            spectrum[drive, rows, :] = value * inverse
        return 0

    lax.fori_loop(0, N // CHUNK, body, 0)


ROWS = 32


def eigen_stress(conc):
    rise = (3.0 * FIRST_RISE + 2.0 * SHEAR_RISE) * EIGEN_STRAIN
    low = (3.0 * FIRST_LOW + 2.0 * SHEAR_LOW) * EIGEN_STRAIN
    return (0.5 - conc) * (rise * (conc + 0.5) + low)


def polarize(parts, conc):
    first = FIRST_LOW + FIRST_RISE * conc
    excess = 2.0 * (SHEAR_LOW + SHEAR_RISE * conc - SHEAR_REF)
    normal = (first - FIRST_REF) * (parts[0] + parts[1] + parts[2]) + eigen_stress(conc)
    return [normal + excess * p for p in parts[:3]] + [excess * p for p in parts[3:]]


def potential(parts, conc):
    first = FIRST_LOW + FIRST_RISE * conc
    shear = SHEAR_LOW + SHEAR_RISE * conc
    dilation = EIGEN_STRAIN * conc
    d = [p - dilation for p in parts[:3]]
    trace = d[0] + d[1] + d[2]
    energy = d[0] * d[0] + d[1] * d[1] + d[2] * d[2]
    energy = energy + 2.0 * (parts[3] * parts[3] + parts[4] * parts[4] + parts[5] * parts[5])
    chemical = 2.0 * WELL_HEIGHT * conc * (1.0 - conc) * (1.0 - 2.0 * conc)
    return (
        chemical
        + 0.5 * FIRST_RISE * trace * trace
        + SHEAR_RISE * energy
        - EIGEN_STRAIN * (3.0 * first + 2.0 * shear) * trace
    )


def sum_squares(parts):
    total = parts[0] * parts[0]
    for part in parts[1:]:
        total = total + part * part
    return total


def fold(value):
    tile = value[0:8, 0:H] + value[0:8, H:N]
    for at in range(8, ROWS, 8):
        tile = tile + (value[at : at + 8, 0:H] + value[at : at + 8, H:N])
    return tile


ORDER = (XX, XY, XZ, YY, YZ, ZZ)
PRESSURE, CONC, FIRST, STRESS, SHIFT, DRIVE, NEXT = 0, 1, 2, 5, 10, 15, 16
FIELDS = 17
COLS, LINES = 16, 8
MESH = pl.DeviceIdType.MESH


def step_kernel(
    base,
    concentration,
    result,
    strain_out,
    norms,
    landed,
    sent,
    plain,
    conc,
    work,
    before,
    turned,
    spectrum,
    conc_hat,
    planes,
    lines,
    tall,
    wide,
    zf,
    zb,
    yf,
    yb,
    xf,
    xb,
    partial,
    col_sums,
    row_sums,
    send_sems,
    recv_sems,
    side_send,
    side_recv,
):
    row, col = lax.axis_index("row"), lax.axis_index("col")
    me = row * COLS + col
    next_col = lax.rem(col + 1, COLS)

    def tiles(ref, field, device):
        return ref.at[field, pl.ds(pl.multiple_of(device * 8, 8), 8), :]

    def send(field):
        def go(i, _):
            other = lax.rem(me + i, 128)
            pltpu.make_async_remote_copy(
                src_ref=tiles(sent, field, other),
                dst_ref=tiles(landed, field, me),
                send_sem=send_sems.at[field],
                recv_sem=recv_sems.at[field],
                device_id=(other // COLS, lax.rem(other, COLS)),
                device_id_type=MESH,
            ).start()
            return 0

        lax.fori_loop(1, 128, go, 0)
        own = pl.ds(pl.multiple_of(me * 8, 8), 8)
        landed[field, own, :] = sent[field, own, :]

    def whole(field):
        rows = pl.ds(0, 127 * 8)
        return pltpu.make_async_remote_copy(
            src_ref=sent.at[field, rows, :],
            dst_ref=landed.at[field, rows, :],
            send_sem=send_sems.at[field],
            recv_sem=recv_sems.at[field],
            device_id=(row, next_col),
            device_id_type=MESH,
        )

    def receive(field):
        whole(field).wait_recv()

    def column_copy(src_of, dst, index, target):
        return pltpu.make_async_remote_copy(
            src_ref=src_of(target),
            dst_ref=dst,
            send_sem=side_send.at[index],
            recv_sem=side_recv.at[index],
            device_id=(row, target),
            device_id_type=MESH,
        )

    def column_send(src_of, dst, index):
        def go(i, _):
            column_copy(src_of, dst, index, lax.rem(col + i, COLS)).start()
            return 0

        lax.fori_loop(1, COLS, go, 0)

    def lines_of(device):
        return pl.ds(pl.multiple_of(device * 16, 16), 16)

    def pair_of(device):
        return pl.ds(device * 2, 2)

    column_send(lambda t: concentration.at[pair_of(t)], plain.at[:, lines_of(col), :], 0)
    plain[:, lines_of(col), :] = concentration[pair_of(col)]
    fill_z_ahead(base, zf)
    fill_z_back(base, zb)
    fill_right(base, yf, -1)
    fill_right(base, yb, 1)
    fill_left(base, xf, 1)
    fill_left(base, xb, -1)

    def arrived(src, dst, index):
        return pltpu.make_async_remote_copy(
            src_ref=src,
            dst_ref=dst,
            send_sem=side_send.at[index],
            recv_sem=side_recv.at[index],
            device_id=(row, next_col),
            device_id_type=MESH,
        )

    arrived(concentration.at[pl.ds(0, 30)], plain.at[:, pl.ds(0, 240), :], 0).wait_recv()
    for x in range(2):
        conc[x] = plain[x].T

    def first_ahead(k, _):
        def choose(chunk, _):
            rows = pl.ds(chunk * ROWS, ROWS)
            for x in range(2):
                value = conc[x, rows, :]
                work[0, x, rows, :] = jnp.where(k == 0, eigen_stress(value), value)
            return 0

        lax.fori_loop(0, N // ROWS, choose, 0)
        ahead(0)
        store_planes(sent, PRESSURE + k, lines)
        send(PRESSURE + k)
        return 0

    def ahead(slot):
        for x in range(2):
            z_ahead(work[slot, x], zf, tall, wide, x)
        lines[...] = dot(wide[...], yf[...])

    lax.fori_loop(0, 2, first_ahead, 0)

    receive(PRESSURE)
    x_ahead(landed, PRESSURE, xf, tall, spectrum, 3)
    green_first(spectrum, 3, me)

    def first_back(slot, _):
        x_back(spectrum, slot, xb, tall, sent, FIRST + slot)
        send(FIRST + slot)
        return 0

    lax.fori_loop(0, 3, first_back, 0)
    receive(CONC)
    x_ahead(landed, CONC, xf, tall, spectrum, 3)
    conc_hat[...] = spectrum[3]

    wave_y, wave_z = lane_wave(H), row_wave_z()

    def put(x, real, imag, factor=None):
        if factor is not None:
            real, imag = factor * real, factor * imag
        put_pair(wide, x, real, imag)

    def back(slot):
        lines[...] = dot(wide[...], yb[...])
        for x in range(2):
            rows = slice(x * H, (x + 1) * H)
            work[slot, x] = z_back(lines[rows, 0:N], lines[rows, N : 2 * N], zb, tall)

    def first_strain(k, _):
        for slot, field, factor in (
            (0, 0, None),
            (1, 1, wave_y),
            (2, 1, wave_z),
            (3, 2, wave_y * wave_y),
            (4, 2, wave_y * wave_z),
            (5, 2, wave_z * wave_z),
        ):

            @pl.when(k == slot)
            def _():
                if slot in (0, 1, 3):
                    receive(FIRST + field)
                for x in range(2):
                    put(x, *load_plane(landed, FIRST + field, x), factor)

        back(k)
        return 0

    lax.fori_loop(0, 6, first_strain, 0)
    partial[...] = jnp.zeros_like(partial)

    def stress(chunk, _):
        rows = pl.ds(chunk * ROWS, ROWS)
        for x in range(2):
            parts = [work[i, x, rows, :] for i in range(6)]
            for i in range(6):
                before[i, x, rows, :] = parts[i]
            partial[0] += sum_squares(parts)
            xx, xy, xz, yy, yz, zz = parts
            value = polarize([xx, yy, zz, yz, xz, xy], conc[x, rows, :])
            for i, which in enumerate(ORDER):
                work[i, x, rows, :] = value[which]
        return 0

    lax.fori_loop(0, N // ROWS, stress, 0)

    def stress_ahead(k, _):
        ahead(k)

        @pl.when(k >= 3)
        def _():
            def mix(chunk, _):
                rows = pl.ds(chunk * ROWS, ROWS)
                index = chunk * ROWS + lax.broadcasted_iota(jnp.int32, (ROWS, N), 0)
                along_z = jnp.where(index < H, index, index - H).astype(F32) * STEP
                along_y = lane_wave(ROWS)
                for part in range(2):
                    lanes = slice(part * N, (part + 1) * N)
                    value = lines[rows, lanes]
                    lines[rows, lanes] = planes[rows, lanes] + along_z * value
                    planes[rows, lanes] = along_y * value
                return 0

            lax.fori_loop(0, N // ROWS, mix, 0)

        @pl.when(k != 3)
        def _():
            field = STRESS + jnp.where(k < 3, k, k - 1)
            store_planes(sent, field, lines)
            send(field)

        return 0

    planes[...] = jnp.zeros_like(planes)
    lax.fori_loop(0, 6, stress_ahead, 0)

    def stress_x(slot, _):
        receive(STRESS + slot)
        x_ahead(landed, STRESS + slot, xf, tall, spectrum, slot)
        return 0

    lax.fori_loop(0, 5, stress_x, 0)
    green_full(spectrum, me)

    def shift_x(slot, _):
        x_back(spectrum, slot, xb, tall, sent, SHIFT + slot)
        send(SHIFT + slot)
        return 0

    lax.fori_loop(0, 5, shift_x, 0)

    def second_strain(k, _):
        for slot, field, factor in (
            (0, 0, None),
            (1, 1, None),
            (2, 2, None),
            (3, 3, wave_y),
            (5, 4, wave_z),
        ):

            @pl.when(k == slot)
            def _():
                if slot < 4:
                    receive(SHIFT + field)
                for x in range(2):
                    put(x, *load_plane(landed, SHIFT + field, x), factor)

        @pl.when(k == 4)
        def _():
            receive(SHIFT + 4)
            for x in range(2):
                real_y, imag_y = load_plane(landed, SHIFT + 3, x)
                real_z, imag_z = load_plane(landed, SHIFT + 4, x)
                put(
                    x,
                    0.5 * (wave_y * real_z + wave_z * real_y),
                    0.5 * (wave_y * imag_z + wave_z * imag_y),
                )

        back(k)
        for x in range(2):
            turned[k, x] = work[k, x].T
        return 0

    lax.fori_loop(0, 6, second_strain, 0)

    def drive(chunk, _):
        rows = pl.ds(chunk * ROWS, ROWS)
        for x in range(2):
            parts = [work[i, x, rows, :] for i in range(6)]
            partial[1] += sum_squares([p - before[i, x, rows, :] for i, p in enumerate(parts)])
            xx, xy, xz, yy, yz, zz = parts
            work[0, x, rows, :] = potential([xx, yy, zz, yz, xz, xy], conc[x, rows, :])
        return 0

    lax.fori_loop(0, N // ROWS, drive, 0)
    ahead(0)
    store_planes(sent, DRIVE, lines)
    send(DRIVE)

    def strain_send(slots):
        for slot in slots:
            column_send(
                lambda t: turned.at[slot, :, lines_of(t), :],
                strain_out.at[ORDER[slot], pair_of(col)],
                1 + slot,
            )
            own = pltpu.make_async_copy(
                turned.at[slot, :, lines_of(col), :],
                strain_out.at[ORDER[slot], pair_of(col)],
                side_send.at[9 + slot],
            )
            own.start()

    col_sums[col, 0:8, :] = fold(partial[0])
    col_sums[col, 8:16, :] = fold(partial[1])
    column_send(lambda t: col_sums.at[col], col_sums.at[col], 8)
    strain_send((0, 1))

    receive(DRIVE)
    x_ahead(landed, DRIVE, xf, tall, spectrum, 0)
    relax(spectrum, 0, conc_hat, me)
    x_back(spectrum, 0, xb, tall, sent, NEXT)
    send(NEXT)
    strain_send((2, 3))

    arrived(col_sums.at[pl.ds(0, 15)], col_sums.at[pl.ds(0, 15)], 8).wait_recv()
    total = col_sums[0]
    for i in range(1, COLS):
        total = total + col_sums[i]
    row_sums[row] = total

    def row_send(i, _):
        pltpu.make_async_remote_copy(
            src_ref=row_sums.at[row],
            dst_ref=row_sums.at[row],
            send_sem=side_send.at[15],
            recv_sem=side_recv.at[15],
            device_id=(lax.rem(row + i, LINES), col),
            device_id_type=MESH,
        ).start()
        return 0

    lax.fori_loop(1, LINES, row_send, 0)

    receive(NEXT)
    for x in range(2):
        put(x, *load_plane(landed, NEXT, x))
    back(0)
    for x in range(2):
        work[1, x] = work[0, x].T
    column_send(lambda t: work.at[1, :, lines_of(t), :], result.at[pair_of(col)], 7)
    own = pltpu.make_async_copy(
        work.at[1, :, lines_of(col), :], result.at[pair_of(col)], side_send.at[16]
    )
    own.start()
    strain_send((4, 5))

    row_wait = pltpu.make_async_remote_copy(
        src_ref=row_sums.at[pl.ds(0, LINES - 1)],
        dst_ref=row_sums.at[pl.ds(0, LINES - 1)],
        send_sem=side_send.at[15],
        recv_sem=side_recv.at[15],
        device_id=(lax.rem(row + 1, LINES), col),
        device_id_type=MESH,
    )
    row_wait.wait_recv()
    total = row_sums[0]
    for i in range(1, LINES):
        total = total + row_sums[i]
    norms[...] = total
    row_wait.wait_send()

    def sent_all(field, _):
        whole(field).wait_send()
        return 0

    lax.fori_loop(0, FIELDS, sent_all, 0)
    arrived(concentration.at[pl.ds(0, 30)], plain.at[:, pl.ds(0, 240), :], 0).wait_send()
    arrived(col_sums.at[pl.ds(0, 15)], col_sums.at[pl.ds(0, 15)], 8).wait_send()
    for slot in range(6):
        both = arrived(turned.at[slot, :, pl.ds(0, 240), :], strain_out.at[ORDER[slot], pl.ds(0, 30)], 1 + slot)
        both.wait_send()
        both.wait_recv()
        pltpu.make_async_copy(
            turned.at[slot, :, lines_of(col), :],
            strain_out.at[ORDER[slot], pair_of(col)],
            side_send.at[9 + slot],
        ).wait()
    both = arrived(work.at[1, :, pl.ds(0, 240), :], result.at[pl.ds(0, 30)], 7)
    both.wait_send()
    both.wait_recv()
    own.wait()


def shape(*dims):
    return jax.ShapeDtypeStruct(dims, F32)


def shards(base, concentration):
    vmem = pl.BlockSpec(memory_space=pltpu.VMEM)
    hbm = pl.BlockSpec(memory_space=pl.ANY)
    result, strain, norms = pl.pallas_call(
        step_kernel,
        out_shape=[shape(32, 16, N), shape(6, 32, 16, N), shape(16, H)],
        in_specs=[vmem, vmem],
        out_specs=[hbm, hbm, vmem],
        scratch_shapes=[
            pltpu.VMEM((FIELDS, 8 * H, H), F32),
            pltpu.VMEM((FIELDS, 8 * H, H), F32),
            pltpu.VMEM((2, N, N), F32),
            pltpu.VMEM((2, N, N), F32),
            pltpu.VMEM((6, 2, N, N), F32),
            pltpu.VMEM((6, 2, N, N), F32),
            pltpu.VMEM((6, 2, N, N), F32),
            pltpu.VMEM((5, 2 * N, N), F32),
            pltpu.VMEM((2 * N, N), F32),
            pltpu.VMEM((N, 2 * N), F32),
            pltpu.VMEM((N, 2 * N), F32),
            pltpu.VMEM((6 * N, N), B16),
            pltpu.VMEM((2 * H, 6 * N), B16),
            pltpu.VMEM((N, 3 * N), B16),
            pltpu.VMEM((N, 3 * N), B16),
            pltpu.VMEM((6 * N, 2 * N), B16),
            pltpu.VMEM((6 * N, 2 * N), B16),
            pltpu.VMEM((2 * N, 6 * N), B16),
            pltpu.VMEM((2 * N, 6 * N), B16),
            pltpu.VMEM((2, ROWS, N), F32),
            pltpu.VMEM((COLS, 16, H), F32),
            pltpu.VMEM((LINES, 16, H), F32),
            pltpu.SemaphoreType.DMA((FIELDS,)),
            pltpu.SemaphoreType.DMA((FIELDS,)),
            pltpu.SemaphoreType.DMA((17,)),
            pltpu.SemaphoreType.DMA((17,)),
        ],
        compiler_params=pltpu.CompilerParams(
            vmem_limit_bytes=60 * 2**20, has_side_effects=True
        ),
        name="step",
    )(base, concentration)
    sums = jnp.sum(norms.reshape(2, 8 * H), axis=1)
    return result, strain, jnp.sqrt(sums * SCALE)


def solution(mesh):
    base = base_tables()
    body = jax.shard_map(
        shards,
        mesh=mesh,
        in_specs=(P(), P("row", "col", None)),
        out_specs=(P("row", "col", None), P(None, "row", "col", None), P()),
        check_vma=False,
    )

    def run(concentration):
        return body(jnp.asarray(base), concentration)

    return run
```

time: 385 us -> 204 us (0.53)
  blocking collectives: 288 us -> 0 us
  Pallas kernels: 54.1 us -> 195 us
  local copies, waits for them, and re-layouts: 23.6 us -> 6.08 us
  starting transfers between devices: 7.99 us -> 0 us
  waiting for transfers between devices: 6.69 us -> 0 us
    all_to_all x7 -> x0, blocking collectives: 191 us -> none  [the longest x6 172 us: exchange(): data = lax.all_to_all(data, ALL, split_axis=1, concat_axis=1, tiled=True)]
    pallas_call x7 -> x1, Pallas kernels: 54.1 us -> 195 us  [shards(): pl.pallas_call(step_kernel, out_shape=[shape(32, 16, N), shape(6, 32, 16,...]
    psum x1 -> x0, blocking collectives: 96.2 us -> none  [shards(): sums = lax.psum(jnp.stack([jnp.sum(first), jnp.sum(second)]), ALL)]
    all_to_all x7 -> x0, local copies, waits for them, and re-layouts: 10.7 us -> none  [the longest x4 5.68 us: exchange(): data = lax.all_to_all(data, ALL, split_axis=1, concat_axis=1, tiled=True)]
    all_to_all x2 -> x0, starting transfers between devices: 7.99 us -> none  [the longest x1 4.25 us: shards(): lax.all_to_all(plain, 'col', split_axis=1, concat_axis=0, tiled=True)]
    all_to_all x2 -> x0, waiting for transfers between devices: 6.69 us -> none  [the longest x1 6.69 us: shards(): lax.all_to_all(plain, 'col', split_axis=1, concat_axis=0, tiled=True)]
    reshape x4 -> x0, local copies, waits for them, and re-layouts: 6.62 us -> none  [exchange(): data = data.reshape(fields, H, 8, H)]
    pallas_call x2 -> x0, local copies, waits for them, and re-layouts: 6.34 us -> none  [call(): pl.pallas_call(body, out_shape=outs, in_specs=[vmem] * len(args), out_spe...]
  transfers between devices with their start and end apart: 2 -> 0, of which waited for: 1 -> 0; matrix products, arithmetic and copies ran while one was open for 2% -> 0% of each run, Pallas kernels for 0% -> 0%
where the time goes in v2:
time: 204 us; the launch traced here: 203 us
  Pallas kernels  195 us (96%)
  local copies, waits for them, and re-layouts  6.08 us (3%)
    pallas_call x1, Pallas kernels, shards(): pl.pallas_call(step_kernel, out_shape=[shape(32, 16, N), shape(6, 32, 16,...  195 us
    unnamed x2, local copies, waits for them, and re-layouts  6 us

profile of v2, /device:TPU:1, one launch (start us, length us, event | category | flops | bytes accessed | tf_op | source)
XLA Modules:
  0.0 203.5 jit_solution(4185258008238033289)
XLA Ops:
  0.6 195.3 %step.1 = (f32[32,16,256]{2,1,0:T(8,128)}, f32[6,32,16,256]{3,2,1,0:T(8,128)}, f32[16,128]{1,0:T(8,128)}) custom-call(bf16[4,256,256]{2,1,0:T(8,128)(2,1)} %constant.6.clone.base, f32[32,16,256]{2,1,0:T(8,128)} %concentration.1), custom_call_target="tpu_custom_call" | custom-call | tf_op jit(solution)/shard_map/step/pallas_call | solution.py:693
  195.9 0.8 reduce_sum.10
  196.7 0.1 reduce_sum.14
  196.8 0.1 reduce_sum.18
  196.9 0.5 multiply_sqrt_fusion
  197.5 1.9 copy.7
  199.3 4.1 %copy.8 = f32[6,32,16,256]{3,2,1,0:T(8,128)} copy(f32[6,32,16,256]{3,2,1,0:T(8,128)} %get-tuple-element.13) | data formatting | bytes 6291456

commit v3 on v2

--- a/solution.py
+++ b/solution.py
@@ -99,13 +99,12 @@
         wide[rows, 4 * N + at : 5 * N + at] = lead
 
 
-def z_ahead(field, z_table, tall, wide, x):
+def z_ahead(field, z_table, tall):
     lead, rest = split(field)
     tall[0:N, :] = lead
     tall[N : 2 * N, :] = rest
     tall[2 * N : 3 * N, :] = lead
-    spectrum = dot(z_table[...], tall[0 : 3 * N, :])
-    put_pair(wide, x, spectrum[0:H], spectrum[H:N])
+    return dot(z_table[...], tall[0 : 3 * N, :])
 
 
 def z_back(real, imag, z_table, tall):
@@ -130,29 +129,83 @@
     return jnp.concatenate(parts[0:2], axis=1), jnp.concatenate(parts[2:4], axis=1)
 
 
+def put_tall(tall, part, rows, lanes):
+    lead, rest = split(rows)
+    at = part * N
+    tall[at : at + N, lanes] = lead
+    tall[2 * N + at : 3 * N + at, lanes] = rest
+    tall[4 * N + at : 5 * N + at, lanes] = lead
+
+
 def x_ahead(landed, field, x_table, tall, spectrum, slot):
     for part in range(2):
         for half in range(2):
             rows = landed[field, pl.ds(part * 2 + half, N, stride=4), :]
-            lead, rest = split(rows)
-            at, lanes = part * N, slice(half * H, (half + 1) * H)
-            tall[at : at + N, lanes] = lead
-            tall[2 * N + at : 3 * N + at, lanes] = rest
-            tall[4 * N + at : 5 * N + at, lanes] = lead
+            put_tall(tall, part, rows, slice(half * H, (half + 1) * H))
     spectrum[slot] = dot(x_table[...], tall[...])
 
 
-def x_back(spectrum, slot, x_table, tall, out, field):
-    lead, rest = split(spectrum[slot])
-    tall[0 : 2 * N, :] = lead
-    tall[2 * N : 4 * N, :] = rest
-    tall[4 * N : 6 * N, :] = lead
-    lines = dot(x_table[...], tall[...])
+def x_lines(source, x_table, tall):
+    for part in range(2):
+        put_tall(tall, part, source[part * N : (part + 1) * N], slice(0, N))
+    return dot(x_table[...], tall[...])
+
+
+def store_lines(out, field, lines):
     for part in range(2):
         for half in range(2):
             out[field, pl.ds(part * 2 + half, N, stride=4), :] = lines[
                 part * N : (part + 1) * N, half * H : (half + 1) * H
             ]
+
+
+def put_rows(wide, rows, at, value):
+    lead, rest = split(value)
+    count = value.shape[1]
+    wide[rows, at : at + count] = lead
+    wide[rows, 2 * N + at : 2 * N + at + count] = rest
+    wide[rows, 4 * N + at : 4 * N + at + count] = lead
+
+
+def turn_groups(value):
+    row = lax.broadcasted_iota(jnp.int32, value.shape, 1)
+    group = lax.broadcasted_iota(jnp.int32, value.shape, 2) // 16
+    for bit in (1, 2, 4):
+        row_set, group_set = (row & bit) != 0, (group & bit) != 0
+        above = pltpu.roll(pltpu.roll(value, 8 - bit, axis=1), 16 * bit, axis=2)
+        below = pltpu.roll(pltpu.roll(value, bit, axis=1), H - 16 * bit, axis=2)
+        value = jnp.where(row_set == group_set, value, jnp.where(group_set, above, below))
+    return value
+
+
+def tile_rows(block, part, high, which):
+    return pl.ds(block * H + high * 64 + part * 4 + which, 8, stride=8)
+
+
+def gather_cells(landed, field, wide):
+    def go(block, _):
+        for part in range(2):
+            for high in range(2):
+                parts = [landed[field, tile_rows(block, part, high, i), :] for i in range(4)]
+                value = turn_groups(jnp.stack(parts)).reshape(32, H)
+                put_rows(wide, pl.ds(block * 32, 32), part * N + high * H, value)
+        return 0
+
+    lax.fori_loop(0, 8, go, 0)
+
+
+def scatter_cells(out, field, lines):
+    def go(block, _):
+        for part in range(2):
+            for high in range(2):
+                at = part * N + high * H
+                value = lines[pl.ds(block * 32, 32), at : at + H].reshape(4, 8, H)
+                value = turn_groups(value)
+                for i in range(4):
+                    out[field, tile_rows(block, part, high, i), :] = value[i]
+        return 0
+
+    lax.fori_loop(0, 8, go, 0)
 
 
 def signed(index):
@@ -214,11 +267,12 @@
             moved_x = scale * (force_x - along * wave_x)
             moved_y = scale * (force_y - along * wave_y)
             moved_z = scale * (force_z - along * wave_z)
-            spectrum[0, rows, :] = wave_x * moved_x
-            spectrum[1, rows, :] = 0.5 * (wave_x * moved_y + wave_y * moved_x)
-            spectrum[2, rows, :] = 0.5 * (wave_x * moved_z + wave_z * moved_x)
-            spectrum[3, rows, :] = moved_y
-            spectrum[4, rows, :] = moved_z
+            spectrum[XX, rows, :] = wave_x * moved_x
+            spectrum[YY, rows, :] = wave_y * moved_y
+            spectrum[ZZ, rows, :] = wave_z * moved_z
+            spectrum[YZ, rows, :] = 0.5 * (wave_y * moved_z + wave_z * moved_y)
+            spectrum[XZ, rows, :] = 0.5 * (wave_x * moved_z + wave_z * moved_x)
+            spectrum[XY, rows, :] = 0.5 * (wave_x * moved_y + wave_y * moved_x)
         return 0
 
     lax.fori_loop(0, N // CHUNK, body, 0)
@@ -285,8 +339,8 @@
 
 
 ORDER = (XX, XY, XZ, YY, YZ, ZZ)
-PRESSURE, CONC, FIRST, STRESS, SHIFT, DRIVE, NEXT = 0, 1, 2, 5, 10, 15, 16
-FIELDS = 17
+PRESSURE, CONC, FIRST, STRESS, SHIFT, DRIVE, NEXT = 0, 1, 2, 5, 10, 16, 17
+FIELDS = 18
 COLS, LINES = 16, 8
 MESH = pl.DeviceIdType.MESH
 
@@ -300,9 +354,11 @@
     landed,
     sent,
     plain,
+    cells,
     conc,
     work,
     before,
+    kept,
     turned,
     spectrum,
     conc_hat,
@@ -362,99 +418,101 @@
     def receive(field):
         whole(field).wait_recv()
 
-    def column_copy(src_of, dst, index, target):
-        return pltpu.make_async_remote_copy(
-            src_ref=src_of(target),
-            dst_ref=dst,
-            send_sem=side_send.at[index],
-            recv_sem=side_recv.at[index],
-            device_id=(row, target),
-            device_id_type=MESH,
-        )
-
-    def column_send(src_of, dst, index):
-        def go(i, _):
-            column_copy(src_of, dst, index, lax.rem(col + i, COLS)).start()
-            return 0
-
-        lax.fori_loop(1, COLS, go, 0)
-
-    def lines_of(device):
-        return pl.ds(pl.multiple_of(device * 16, 16), 16)
-
-    def pair_of(device):
-        return pl.ds(device * 2, 2)
-
-    column_send(lambda t: concentration.at[pair_of(t)], plain.at[:, lines_of(col), :], 0)
-    plain[:, lines_of(col), :] = concentration[pair_of(col)]
-    fill_z_ahead(base, zf)
-    fill_z_back(base, zb)
-    fill_right(base, yf, -1)
-    fill_right(base, yb, 1)
-    fill_left(base, xf, 1)
-    fill_left(base, xb, -1)
-
-    def arrived(src, dst, index):
+    def side_copy(src, dst, index, device):
         return pltpu.make_async_remote_copy(
             src_ref=src,
             dst_ref=dst,
             send_sem=side_send.at[index],
             recv_sem=side_recv.at[index],
-            device_id=(row, next_col),
+            device_id=device,
             device_id_type=MESH,
         )
 
-    arrived(concentration.at[pl.ds(0, 30)], plain.at[:, pl.ds(0, 240), :], 0).wait_recv()
+    def column_send(src_of, dst, index):
+        def go(i, _):
+            target = lax.rem(col + i, COLS)
+            side_copy(src_of(target), dst, index, (row, target)).start()
+            return 0
+
+        lax.fori_loop(1, COLS, go, 0)
+
+    def lines_of(device):
+        return pl.ds(pl.multiple_of(device * 16, 16), 16)
+
+    def pair_of(device):
+        return pl.ds(device * 2, 2)
+
+
+    def cells_ahead(field, field_of):
+        for half in range(2):
+            value = z_ahead(field_of(half), zf, tall)
+            for part in range(2):
+                for j in range(2):
+                    sent[field, pl.ds(part * 4 + 2 * half + j, H, stride=8), :] = value[
+                        part * H : (part + 1) * H, j * H : (j + 1) * H
+                    ]
+
+    def cells_back(field, half):
+        parts = [landed[field, pl.ds(i, H, stride=8), :] for i in range(8)]
+        real = jnp.concatenate(parts[2 * half : 2 * half + 2], axis=1)
+        imag = jnp.concatenate(parts[4 + 2 * half : 6 + 2 * half], axis=1)
+        return z_back(real, imag, zb, tall)
+
+    def plane_ahead(field, slot):
+        gather_cells(landed, field, wide)
+        lines[...] = dot(wide[...], yf[...])
+        for part in range(2):
+            put_tall(tall, part, lines[:, part * N : (part + 1) * N], slice(0, N))
+        spectrum[slot] = dot(xf[...], tall[...])
+
+    def plane_lines(value, factor=None):
+        for part in range(2):
+            rows = value[part * N : (part + 1) * N]
+            if factor is not None:
+                rows = factor * rows
+            put_rows(wide, slice(0, N), part * N, rows)
+
+    def plane_back():
+        lines[...] = dot(wide[...], yb[...])
+
+    fill_z_ahead(base, zf)
+    for half in range(2):
+        block = concentration[16 * half : 16 * half + 16].reshape(N, N)
+        cells[half] = block.T
+
+    def first_pressure(half):
+        return eigen_stress(cells[half])
+
+    cells_ahead(PRESSURE, first_pressure)
+    send(PRESSURE)
+    column_send(lambda t: concentration.at[pair_of(t)], plain.at[:, lines_of(col), :], 0)
+    plain[:, lines_of(col), :] = concentration[pair_of(col)]
+    plain_src, plain_dst = concentration.at[pl.ds(0, 30)], plain.at[:, pl.ds(0, 240), :]
+    plain_wait = side_copy(plain_src, plain_dst, 0, (row, next_col))
+    fill_right(base, yf, -1)
+    fill_left(base, xf, 1)
+    fill_left(base, xb, -1)
+    fill_z_back(base, zb)
+    fill_right(base, yb, 1)
+    cells_ahead(CONC, lambda half: cells[half])
+
+    receive(PRESSURE)
+    plane_ahead(PRESSURE, 3)
+    green_first(spectrum, 3, me)
+
+    def first_back(slot, _):
+        kept[slot] = x_lines(spectrum.at[slot], xb, tall)
+        store_lines(sent, FIRST + slot, kept.at[slot])
+        send(FIRST + slot)
+        return 0
+
+    lax.fori_loop(0, 3, first_back, 0)
+    send(CONC)
+    plain_wait.wait_recv()
     for x in range(2):
         conc[x] = plain[x].T
 
-    def first_ahead(k, _):
-        def choose(chunk, _):
-            rows = pl.ds(chunk * ROWS, ROWS)
-            for x in range(2):
-                value = conc[x, rows, :]
-                work[0, x, rows, :] = jnp.where(k == 0, eigen_stress(value), value)
-            return 0
-
-        lax.fori_loop(0, N // ROWS, choose, 0)
-        ahead(0)
-        store_planes(sent, PRESSURE + k, lines)
-        send(PRESSURE + k)
-        return 0
-
-    def ahead(slot):
-        for x in range(2):
-            z_ahead(work[slot, x], zf, tall, wide, x)
-        lines[...] = dot(wide[...], yf[...])
-
-    lax.fori_loop(0, 2, first_ahead, 0)
-
-    receive(PRESSURE)
-    x_ahead(landed, PRESSURE, xf, tall, spectrum, 3)
-    green_first(spectrum, 3, me)
-
-    def first_back(slot, _):
-        x_back(spectrum, slot, xb, tall, sent, FIRST + slot)
-        send(FIRST + slot)
-        return 0
-
-    lax.fori_loop(0, 3, first_back, 0)
-    receive(CONC)
-    x_ahead(landed, CONC, xf, tall, spectrum, 3)
-    conc_hat[...] = spectrum[3]
-
     wave_y, wave_z = lane_wave(H), row_wave_z()
-
-    def put(x, real, imag, factor=None):
-        if factor is not None:
-            real, imag = factor * real, factor * imag
-        put_pair(wide, x, real, imag)
-
-    def back(slot):
-        lines[...] = dot(wide[...], yb[...])
-        for x in range(2):
-            rows = slice(x * H, (x + 1) * H)
-            work[slot, x] = z_back(lines[rows, 0:N], lines[rows, N : 2 * N], zb, tall)
 
     def first_strain(k, _):
         for slot, field, factor in (
@@ -471,9 +529,15 @@
                 if slot in (0, 1, 3):
                     receive(FIRST + field)
                 for x in range(2):
-                    put(x, *load_plane(landed, FIRST + field, x), factor)
-
-        back(k)
+                    real, imag = load_plane(landed, FIRST + field, x)
+                    if factor is not None:
+                        real, imag = factor * real, factor * imag
+                    put_pair(wide, x, real, imag)
+
+        plane_back()
+        for x in range(2):
+            rows = slice(x * H, (x + 1) * H)
+            work[k, x] = z_back(lines[rows, 0:N], lines[rows, N : 2 * N], zb, tall)
         return 0
 
     lax.fori_loop(0, 6, first_strain, 0)
@@ -483,8 +547,6 @@
         rows = pl.ds(chunk * ROWS, ROWS)
         for x in range(2):
             parts = [work[i, x, rows, :] for i in range(6)]
-            for i in range(6):
-                before[i, x, rows, :] = parts[i]
             partial[0] += sum_squares(parts)
             xx, xy, xz, yy, yz, zz = parts
             value = polarize([xx, yy, zz, yz, xz, xy], conc[x, rows, :])
@@ -495,7 +557,10 @@
     lax.fori_loop(0, N // ROWS, stress, 0)
 
     def stress_ahead(k, _):
-        ahead(k)
+        for x in range(2):
+            value = z_ahead(work[k, x], zf, tall)
+            put_pair(wide, x, value[0:H], value[H:N])
+        lines[...] = dot(wide[...], yf[...])
 
         @pl.when(k >= 3)
         def _():
@@ -524,6 +589,30 @@
     planes[...] = jnp.zeros_like(planes)
     lax.fori_loop(0, 6, stress_ahead, 0)
 
+    receive(CONC)
+    plane_ahead(CONC, 0)
+    conc_hat[...] = spectrum[0]
+    along_y, along_z = lane_wave(N), me.astype(F32) * STEP
+
+    def first_planes(k, _):
+        for which, field, factor in (
+            (XX, 0, None),
+            (YY, 2, along_y * along_y),
+            (ZZ, 2, along_z * along_z),
+            (YZ, 2, along_y * along_z),
+            (XZ, 1, along_z),
+            (XY, 1, along_y),
+        ):
+
+            @pl.when(k == which)
+            def _():
+                plane_lines(kept.at[field], factor)
+
+        before[k] = dot(wide[...], yb[...])
+        return 0
+
+    lax.fori_loop(0, 6, first_planes, 0)
+
     def stress_x(slot, _):
         receive(STRESS + slot)
         x_ahead(landed, STRESS + slot, xf, tall, spectrum, slot)
@@ -532,155 +621,108 @@
     lax.fori_loop(0, 5, stress_x, 0)
     green_full(spectrum, me)
 
-    def shift_x(slot, _):
-        x_back(spectrum, slot, xb, tall, sent, SHIFT + slot)
+    real_weight = jnp.where(me == 0, 1.0, 2.0) * float(N)
+    imag_weight = jnp.where(me == 0, 0.0, 2.0) * float(N)
+
+    def shift_back(slot, _):
+        plane_lines(x_lines(spectrum.at[slot], xb, tall))
+        plane_back()
+        scatter_cells(sent, SHIFT + slot, lines)
         send(SHIFT + slot)
-        return 0
-
-    lax.fori_loop(0, 5, shift_x, 0)
+
+        def squares(chunk, _):
+            rows = pl.ds(chunk * ROWS, ROWS)
+            real = lines[rows, 0:N] - before[slot, rows, 0:N]
+            imag = lines[rows, N : 2 * N] - before[slot, rows, N : 2 * N]
+            partial[1] += real_weight * (real * real) + imag_weight * (imag * imag)
+            return 0
+
+        lax.fori_loop(0, N // ROWS, squares, 0)
+        return 0
+
+    lax.fori_loop(0, 6, shift_back, 0)
+
+    col_sums[col, 0:8, :] = fold(partial[0])
+    col_sums[col, 8:16, :] = fold(partial[1])
+    column_send(lambda t: col_sums.at[col], col_sums.at[col], 1)
+    sums_src = col_sums.at[pl.ds(0, COLS - 1)]
+    col_wait = side_copy(sums_src, sums_src, 1, (row, next_col))
+
+    def strain_copy(k):
+        return pltpu.make_async_copy(turned.at[k], strain_out.at[k], side_send.at[3 + k])
 
     def second_strain(k, _):
-        for slot, field, factor in (
-            (0, 0, None),
-            (1, 1, None),
-            (2, 2, None),
-            (3, 3, wave_y),
-            (5, 4, wave_z),
-        ):
-
-            @pl.when(k == slot)
-            def _():
-                if slot < 4:
-                    receive(SHIFT + field)
-                for x in range(2):
-                    put(x, *load_plane(landed, SHIFT + field, x), factor)
-
-        @pl.when(k == 4)
-        def _():
-            receive(SHIFT + 4)
-            for x in range(2):
-                real_y, imag_y = load_plane(landed, SHIFT + 3, x)
-                real_z, imag_z = load_plane(landed, SHIFT + 4, x)
-                put(
-                    x,
-                    0.5 * (wave_y * real_z + wave_z * real_y),
-                    0.5 * (wave_y * imag_z + wave_z * imag_y),
-                )
-
-        back(k)
-        for x in range(2):
-            turned[k, x] = work[k, x].T
+        receive(SHIFT + k)
+        for half in range(2):
+            work[k, half] = cells_back(SHIFT + k, half)
         return 0
 
     lax.fori_loop(0, 6, second_strain, 0)
 
     def drive(chunk, _):
         rows = pl.ds(chunk * ROWS, ROWS)
-        for x in range(2):
-            parts = [work[i, x, rows, :] for i in range(6)]
-            partial[1] += sum_squares([p - before[i, x, rows, :] for i, p in enumerate(parts)])
-            xx, xy, xz, yy, yz, zz = parts
-            work[0, x, rows, :] = potential([xx, yy, zz, yz, xz, xy], conc[x, rows, :])
+        for half in range(2):
+            parts = [work[i, half, rows, :] for i in range(6)]
+            planes[rows, half * N : (half + 1) * N] = potential(parts, cells[half, rows, :])
         return 0
 
     lax.fori_loop(0, N // ROWS, drive, 0)
-    ahead(0)
-    store_planes(sent, DRIVE, lines)
+    cells_ahead(DRIVE, lambda half: planes[:, half * N : (half + 1) * N])
     send(DRIVE)
 
-    def strain_send(slots):
-        for slot in slots:
-            column_send(
-                lambda t: turned.at[slot, :, lines_of(t), :],
-                strain_out.at[ORDER[slot], pair_of(col)],
-                1 + slot,
-            )
-            own = pltpu.make_async_copy(
-                turned.at[slot, :, lines_of(col), :],
-                strain_out.at[ORDER[slot], pair_of(col)],
-                side_send.at[9 + slot],
-            )
-            own.start()
-
-    col_sums[col, 0:8, :] = fold(partial[0])
-    col_sums[col, 8:16, :] = fold(partial[1])
-    column_send(lambda t: col_sums.at[col], col_sums.at[col], 8)
-    strain_send((0, 1))
-
-    receive(DRIVE)
-    x_ahead(landed, DRIVE, xf, tall, spectrum, 0)
-    relax(spectrum, 0, conc_hat, me)
-    x_back(spectrum, 0, xb, tall, sent, NEXT)
-    send(NEXT)
-    strain_send((2, 3))
-
-    arrived(col_sums.at[pl.ds(0, 15)], col_sums.at[pl.ds(0, 15)], 8).wait_recv()
+    def strain_turn(k, _):
+        for half in range(2):
+            turned[k, 16 * half : 16 * half + 16] = work[k, half].T.reshape(16, 16, N)
+        strain_copy(k).start()
+        return 0
+
+    lax.fori_loop(0, 6, strain_turn, 0)
+    col_wait.wait_recv()
     total = col_sums[0]
     for i in range(1, COLS):
         total = total + col_sums[i]
     row_sums[row] = total
 
     def row_send(i, _):
-        pltpu.make_async_remote_copy(
-            src_ref=row_sums.at[row],
-            dst_ref=row_sums.at[row],
-            send_sem=side_send.at[15],
-            recv_sem=side_recv.at[15],
-            device_id=(lax.rem(row + i, LINES), col),
-            device_id_type=MESH,
-        ).start()
+        other = lax.rem(row + i, LINES)
+        side_copy(row_sums.at[row], row_sums.at[row], 2, (other, col)).start()
         return 0
 
     lax.fori_loop(1, LINES, row_send, 0)
-
-    receive(NEXT)
-    for x in range(2):
-        put(x, *load_plane(landed, NEXT, x))
-    back(0)
-    for x in range(2):
-        work[1, x] = work[0, x].T
-    column_send(lambda t: work.at[1, :, lines_of(t), :], result.at[pair_of(col)], 7)
-    own = pltpu.make_async_copy(
-        work.at[1, :, lines_of(col), :], result.at[pair_of(col)], side_send.at[16]
-    )
-    own.start()
-    strain_send((4, 5))
-
-    row_wait = pltpu.make_async_remote_copy(
-        src_ref=row_sums.at[pl.ds(0, LINES - 1)],
-        dst_ref=row_sums.at[pl.ds(0, LINES - 1)],
-        send_sem=side_send.at[15],
-        recv_sem=side_recv.at[15],
-        device_id=(lax.rem(row + 1, LINES), col),
-        device_id_type=MESH,
-    )
+    rows_src = row_sums.at[pl.ds(0, LINES - 1)]
+    row_wait = side_copy(rows_src, rows_src, 2, (lax.rem(row + 1, LINES), col))
+
+    receive(DRIVE)
+    plane_ahead(DRIVE, 0)
+    relax(spectrum, 0, conc_hat, me)
+    plane_lines(x_lines(spectrum.at[0], xb, tall))
+    plane_back()
+    scatter_cells(sent, NEXT, lines)
+    send(NEXT)
+
     row_wait.wait_recv()
     total = row_sums[0]
     for i in range(1, LINES):
         total = total + row_sums[i]
     norms[...] = total
     row_wait.wait_send()
+    col_wait.wait_send()
+    plain_wait.wait_send()
 
     def sent_all(field, _):
         whole(field).wait_send()
         return 0
 
     lax.fori_loop(0, FIELDS, sent_all, 0)
-    arrived(concentration.at[pl.ds(0, 30)], plain.at[:, pl.ds(0, 240), :], 0).wait_send()
-    arrived(col_sums.at[pl.ds(0, 15)], col_sums.at[pl.ds(0, 15)], 8).wait_send()
-    for slot in range(6):
-        both = arrived(turned.at[slot, :, pl.ds(0, 240), :], strain_out.at[ORDER[slot], pl.ds(0, 30)], 1 + slot)
-        both.wait_send()
-        both.wait_recv()
-        pltpu.make_async_copy(
-            turned.at[slot, :, lines_of(col), :],
-            strain_out.at[ORDER[slot], pair_of(col)],
-            side_send.at[9 + slot],
-        ).wait()
-    both = arrived(work.at[1, :, pl.ds(0, 240), :], result.at[pl.ds(0, 30)], 7)
-    both.wait_send()
-    both.wait_recv()
-    own.wait()
+
+    def strain_done(k, _):
+        strain_copy(k).wait()
+        return 0
+
+    lax.fori_loop(0, 6, strain_done, 0)
+    receive(NEXT)
+    for half in range(2):
+        result[16 * half : 16 * half + 16] = cells_back(NEXT, half).T.reshape(16, 16, N)
 
 
 def shape(*dims):
@@ -694,16 +736,18 @@
         step_kernel,
         out_shape=[shape(32, 16, N), shape(6, 32, 16, N), shape(16, H)],
         in_specs=[vmem, vmem],
-        out_specs=[hbm, hbm, vmem],
+        out_specs=[vmem, hbm, vmem],
         scratch_shapes=[
             pltpu.VMEM((FIELDS, 8 * H, H), F32),
             pltpu.VMEM((FIELDS, 8 * H, H), F32),
             pltpu.VMEM((2, N, N), F32),
             pltpu.VMEM((2, N, N), F32),
+            pltpu.VMEM((2, N, N), F32),
             pltpu.VMEM((6, 2, N, N), F32),
-            pltpu.VMEM((6, 2, N, N), F32),
-            pltpu.VMEM((6, 2, N, N), F32),
-            pltpu.VMEM((5, 2 * N, N), F32),
+            pltpu.VMEM((6, N, 2 * N), F32),
+            pltpu.VMEM((3, 2 * N, N), F32),
+            pltpu.VMEM((6, 32, 16, N), F32),
+            pltpu.VMEM((6, 2 * N, N), F32),
             pltpu.VMEM((2 * N, N), F32),
             pltpu.VMEM((N, 2 * N), F32),
             pltpu.VMEM((N, 2 * N), F32),
@@ -720,8 +764,8 @@
             pltpu.VMEM((LINES, 16, H), F32),
             pltpu.SemaphoreType.DMA((FIELDS,)),
             pltpu.SemaphoreType.DMA((FIELDS,)),
-            pltpu.SemaphoreType.DMA((17,)),
-            pltpu.SemaphoreType.DMA((17,)),
+            pltpu.SemaphoreType.DMA((9,)),
+            pltpu.SemaphoreType.DMA((3,)),
         ],
         compiler_params=pltpu.CompilerParams(
             vmem_limit_bytes=60 * 2**20, has_side_effects=True

time: 204 us -> 181 us (0.89)
  Pallas kernels: 195 us -> 173 us
    pallas_call x1, Pallas kernels: 195 us -> 173 us  [shards(): pl.pallas_call(step_kernel, out_shape=[shape(32, 16, N), shape(6, 32, 16,...]
where the time goes in v3:
time: 181 us
  Pallas kernels  173 us (96%)
  local copies, waits for them, and re-layouts  6.08 us (3%)
    pallas_call x1, Pallas kernels, shards(): pl.pallas_call(step_kernel, out_shape=[shape(32, 16, N), shape(6, 32, 16,...  173 us
    unnamed x2, local copies, waits for them, and re-layouts  6 us

profile of v3, /device:TPU:1, one launch (start us, length us, event | category | flops | bytes accessed | tf_op | source)
XLA Modules:
  0.0 180.7 jit_solution(15225213013510949274)
XLA Ops:
  0.6 172.6 %step.1 = (f32[32,16,256]{2,1,0:T(8,128)}, f32[6,32,16,256]{3,2,1,0:T(8,128)}, f32[16,128]{1,0:T(8,128)}) custom-call(bf16[4,256,256]{2,1,0:T(8,128)(2,1)} %constant.6.clone.base, f32[32,16,256]{2,1,0:T(8,128)} %concentration.1), custom_call_target="tpu_custom_call" | custom-call | tf_op jit(solution)/shard_map/step/pallas_call | solution.py:735
  173.2 0.8 reduce_sum.10
  174.0 0.1 reduce_sum.14
  174.1 0.1 reduce_sum.18
  174.2 0.5 multiply_sqrt_fusion
  174.7 1.9 %copy.7 = f32[32,16,256]{2,1,0:T(8,128)} copy(f32[32,16,256]{2,1,0:T(8,128)} %get-tuple-element.12) | data formatting | bytes 1048576
  176.6 4.1 %copy.8 = f32[6,32,16,256]{3,2,1,0:T(8,128)} copy(f32[6,32,16,256]{3,2,1,0:T(8,128)} %get-tuple-element.13) | data formatting | bytes 6291456

commit v4 on v3

--- a/solution.py
+++ b/solution.py
@@ -172,9 +172,11 @@
     group = lax.broadcasted_iota(jnp.int32, value.shape, 2) // 16
     for bit in (1, 2, 4):
         row_set, group_set = (row & bit) != 0, (group & bit) != 0
-        above = pltpu.roll(pltpu.roll(value, 8 - bit, axis=1), 16 * bit, axis=2)
-        below = pltpu.roll(pltpu.roll(value, bit, axis=1), H - 16 * bit, axis=2)
-        value = jnp.where(row_set == group_set, value, jnp.where(group_set, above, below))
+        moved = pltpu.roll(pltpu.roll(value, 8 - bit, axis=1), 16 * bit, axis=2)
+        if bit < 4:
+            below = pltpu.roll(pltpu.roll(value, bit, axis=1), H - 16 * bit, axis=2)
+            moved = jnp.where(group_set, moved, below)
+        value = jnp.where(row_set == group_set, value, moved)
     return value
 
 
@@ -194,18 +196,14 @@
     lax.fori_loop(0, 8, go, 0)
 
 
-def scatter_cells(out, field, lines):
-    def go(block, _):
-        for part in range(2):
-            for high in range(2):
-                at = part * N + high * H
-                value = lines[pl.ds(block * 32, 32), at : at + H].reshape(4, 8, H)
-                value = turn_groups(value)
-                for i in range(4):
-                    out[field, tile_rows(block, part, high, i), :] = value[i]
-        return 0
-
-    lax.fori_loop(0, 8, go, 0)
+def scatter_block(out, field, lines, block):
+    for part in range(2):
+        for high in range(2):
+            at = part * N + high * H
+            value = lines[pl.ds(pl.multiple_of(block * 32, 32), 32), at : at + H]
+            value = turn_groups(value.reshape(4, 8, H))
+            for i in range(4):
+                out[field, tile_rows(block, part, high, i), :] = value[i]
 
 
 def signed(index):
@@ -338,7 +336,7 @@
     return tile
 
 
-ORDER = (XX, XY, XZ, YY, YZ, ZZ)
+ORDER = (YY, YZ, ZZ, XY, XZ, XX)
 PRESSURE, CONC, FIRST, STRESS, SHIFT, DRIVE, NEXT = 0, 1, 2, 5, 10, 16, 17
 FIELDS = 18
 COLS, LINES = 16, 8
@@ -346,11 +344,13 @@
 
 
 def step_kernel(
-    base,
-    concentration,
+    base_hbm,
+    concentration_hbm,
     result,
     strain_out,
     norms,
+    base,
+    concentration,
     landed,
     sent,
     plain,
@@ -387,22 +387,54 @@
     def tiles(ref, field, device):
         return ref.at[field, pl.ds(pl.multiple_of(device * 8, 8), 8), :]
 
-    def send(field):
-        def go(i, _):
-            other = lax.rem(me + i, 128)
+    def row_at(step):
+        return lax.rem(row + step, LINES)
+
+    def each_device(step, act):
+        for shift in range(1 if isinstance(step, int) and step == 0 else 0, COLS):
+            act(row_at(step), lax.rem(col + shift, COLS))
+
+    def send_row(field, step):
+        def go(other_row, other_col):
+            other = other_row * COLS + other_col
             pltpu.make_async_remote_copy(
                 src_ref=tiles(sent, field, other),
                 dst_ref=tiles(landed, field, me),
                 send_sem=send_sems.at[field],
                 recv_sem=recv_sems.at[field],
-                device_id=(other // COLS, lax.rem(other, COLS)),
+                device_id=(other_row, other_col),
                 device_id_type=MESH,
             ).start()
-            return 0
-
-        lax.fori_loop(1, 128, go, 0)
+
+        each_device(step, go)
+
+    def keep_own(field):
         own = pl.ds(pl.multiple_of(me * 8, 8), 8)
         landed[field, own, :] = sent[field, own, :]
+
+    def send(field):
+        send_row(field, 0)
+
+        def go(step, _):
+            send_row(field, step)
+            return 0
+
+        lax.fori_loop(1, LINES, go, 0)
+        keep_own(field)
+
+    def scatter_send(field):
+        scatter_block(sent, field, lines, row)
+        send_row(field, 0)
+        scatter_block(sent, field, lines, row_at(1))
+
+        def go(step, _):
+            send_row(field, step)
+            scatter_block(sent, field, lines, row_at(step + 1))
+            return 0
+
+        lax.fori_loop(1, LINES - 1, go, 0)
+        send_row(field, LINES - 1)
+        keep_own(field)
 
     def whole(field):
         rows = pl.ds(0, 127 * 8)
@@ -475,6 +507,26 @@
     def plane_back():
         lines[...] = dot(wide[...], yb[...])
 
+    concentration_in = pltpu.make_async_copy(concentration_hbm, concentration, side_send.at[10])
+    concentration_in.start()
+    base_in = pltpu.make_async_copy(base_hbm, base, side_send.at[11])
+    base_in.start()
+    barrier = pltpu.get_barrier_semaphore()
+
+    def greet(other_row, other_col):
+        pl.semaphore_signal(
+            barrier, inc=1, device_id=(other_row, other_col), device_id_type=MESH
+        )
+
+    each_device(0, greet)
+
+    def greet_row(step, _):
+        each_device(step, greet)
+        return 0
+
+    lax.fori_loop(1, LINES, greet_row, 0)
+    concentration_in.wait()
+    base_in.wait()
     fill_z_ahead(base, zf)
     for half in range(2):
         block = concentration[16 * half : 16 * half + 16].reshape(N, N)
@@ -484,30 +536,31 @@
         return eigen_stress(cells[half])
 
     cells_ahead(PRESSURE, first_pressure)
+    fill_right(base, yf, -1)
+    fill_left(base, xf, 1)
+    fill_left(base, xb, -1)
+    pl.semaphore_wait(barrier, 127)
     send(PRESSURE)
+    fill_z_back(base, zb)
+    fill_right(base, yb, 1)
+    cells_ahead(CONC, lambda half: cells[half])
+
+    receive(PRESSURE)
     column_send(lambda t: concentration.at[pair_of(t)], plain.at[:, lines_of(col), :], 0)
     plain[:, lines_of(col), :] = concentration[pair_of(col)]
     plain_src, plain_dst = concentration.at[pl.ds(0, 30)], plain.at[:, pl.ds(0, 240), :]
     plain_wait = side_copy(plain_src, plain_dst, 0, (row, next_col))
-    fill_right(base, yf, -1)
-    fill_left(base, xf, 1)
-    fill_left(base, xb, -1)
-    fill_z_back(base, zb)
-    fill_right(base, yb, 1)
-    cells_ahead(CONC, lambda half: cells[half])
-
-    receive(PRESSURE)
     plane_ahead(PRESSURE, 3)
     green_first(spectrum, 3, me)
 
-    def first_back(slot, _):
+    def first_back(step, _):
+        slot = 2 - step
         kept[slot] = x_lines(spectrum.at[slot], xb, tall)
         store_lines(sent, FIRST + slot, kept.at[slot])
         send(FIRST + slot)
         return 0
 
     lax.fori_loop(0, 3, first_back, 0)
-    send(CONC)
     plain_wait.wait_recv()
     for x in range(2):
         conc[x] = plain[x].T
@@ -516,17 +569,17 @@
 
     def first_strain(k, _):
         for slot, field, factor in (
-            (0, 0, None),
-            (1, 1, wave_y),
-            (2, 1, wave_z),
-            (3, 2, wave_y * wave_y),
-            (4, 2, wave_y * wave_z),
-            (5, 2, wave_z * wave_z),
+            (0, 2, wave_y * wave_y),
+            (1, 2, wave_y * wave_z),
+            (2, 2, wave_z * wave_z),
+            (3, 1, wave_y),
+            (4, 1, wave_z),
+            (5, 0, None),
         ):
 
             @pl.when(k == slot)
             def _():
-                if slot in (0, 1, 3):
+                if slot in (0, 3, 5):
                     receive(FIRST + field)
                 for x in range(2):
                     real, imag = load_plane(landed, FIRST + field, x)
@@ -548,7 +601,7 @@
         for x in range(2):
             parts = [work[i, x, rows, :] for i in range(6)]
             partial[0] += sum_squares(parts)
-            xx, xy, xz, yy, yz, zz = parts
+            yy, yz, zz, xy, xz, xx = parts
             value = polarize([xx, yy, zz, yz, xz, xy], conc[x, rows, :])
             for i, which in enumerate(ORDER):
                 work[i, x, rows, :] = value[which]
@@ -557,8 +610,9 @@
     lax.fori_loop(0, N // ROWS, stress, 0)
 
     def stress_ahead(k, _):
+        slot = jnp.where(k == 0, 5, jnp.where(k < 3, k + 2, k - 3))
         for x in range(2):
-            value = z_ahead(work[k, x], zf, tall)
+            value = z_ahead(work[slot, x], zf, tall)
             put_pair(wide, x, value[0:H], value[H:N])
         lines[...] = dot(wide[...], yf[...])
 
@@ -589,9 +643,6 @@
     planes[...] = jnp.zeros_like(planes)
     lax.fori_loop(0, 6, stress_ahead, 0)
 
-    receive(CONC)
-    plane_ahead(CONC, 0)
-    conc_hat[...] = spectrum[0]
     along_y, along_z = lane_wave(N), me.astype(F32) * STEP
 
     def first_planes(k, _):
@@ -627,8 +678,7 @@
     def shift_back(slot, _):
         plane_lines(x_lines(spectrum.at[slot], xb, tall))
         plane_back()
-        scatter_cells(sent, SHIFT + slot, lines)
-        send(SHIFT + slot)
+        scatter_send(SHIFT + slot)
 
         def squares(chunk, _):
             rows = pl.ds(chunk * ROWS, ROWS)
@@ -641,6 +691,7 @@
         return 0
 
     lax.fori_loop(0, 6, shift_back, 0)
+    send(CONC)
 
     col_sums[col, 0:8, :] = fold(partial[0])
     col_sums[col, 8:16, :] = fold(partial[1])
@@ -672,11 +723,14 @@
 
     def strain_turn(k, _):
         for half in range(2):
-            turned[k, 16 * half : 16 * half + 16] = work[k, half].T.reshape(16, 16, N)
+            turned[k, 16 * half : 16 * half + 16] = 2.0 * work[k, half].T.reshape(16, 16, N)
         strain_copy(k).start()
         return 0
 
     lax.fori_loop(0, 6, strain_turn, 0)
+    receive(CONC)
+    plane_ahead(CONC, 0)
+    conc_hat[...] = spectrum[0]
     col_wait.wait_recv()
     total = col_sums[0]
     for i in range(1, COLS):
@@ -697,8 +751,7 @@
     relax(spectrum, 0, conc_hat, me)
     plane_lines(x_lines(spectrum.at[0], xb, tall))
     plane_back()
-    scatter_cells(sent, NEXT, lines)
-    send(NEXT)
+    scatter_send(NEXT)
 
     row_wait.wait_recv()
     total = row_sums[0]
@@ -721,8 +774,18 @@
 
     lax.fori_loop(0, 6, strain_done, 0)
     receive(NEXT)
+    copies = []
     for half in range(2):
-        result[16 * half : 16 * half + 16] = cells_back(NEXT, half).T.reshape(16, 16, N)
+        planes_x = pl.ds(16 * half, 16)
+        turned[0, planes_x] = 2.0 * cells_back(NEXT, half).T.reshape(16, 16, N)
+        copies.append(
+            pltpu.make_async_copy(
+                turned.at[0, planes_x], result.at[planes_x], side_send.at[9 + half]
+            )
+        )
+        copies[-1].start()
+    for copy in copies:
+        copy.wait()
 
 
 def shape(*dims):
@@ -732,12 +795,15 @@
 def shards(base, concentration):
     vmem = pl.BlockSpec(memory_space=pltpu.VMEM)
     hbm = pl.BlockSpec(memory_space=pl.ANY)
+    hbm_in = pl.BlockSpec(memory_space=pltpu.HBM)
     result, strain, norms = pl.pallas_call(
         step_kernel,
         out_shape=[shape(32, 16, N), shape(6, 32, 16, N), shape(16, H)],
-        in_specs=[vmem, vmem],
-        out_specs=[vmem, hbm, vmem],
+        in_specs=[hbm_in, hbm_in],
+        out_specs=[hbm, hbm, vmem],
         scratch_shapes=[
+            pltpu.VMEM((4, N, N), B16),
+            pltpu.VMEM((32, 16, N), F32),
             pltpu.VMEM((FIELDS, 8 * H, H), F32),
             pltpu.VMEM((FIELDS, 8 * H, H), F32),
             pltpu.VMEM((2, N, N), F32),
@@ -764,16 +830,16 @@
             pltpu.VMEM((LINES, 16, H), F32),
             pltpu.SemaphoreType.DMA((FIELDS,)),
             pltpu.SemaphoreType.DMA((FIELDS,)),
-            pltpu.SemaphoreType.DMA((9,)),
+            pltpu.SemaphoreType.DMA((12,)),
             pltpu.SemaphoreType.DMA((3,)),
         ],
         compiler_params=pltpu.CompilerParams(
-            vmem_limit_bytes=60 * 2**20, has_side_effects=True
+            vmem_limit_bytes=48 * 2**20, has_side_effects=True, collective_id=0
         ),
         name="step",
     )(base, concentration)
     sums = jnp.sum(norms.reshape(2, 8 * H), axis=1)
-    return result, strain, jnp.sqrt(sums * SCALE)
+    return 0.5 * result, 0.5 * strain, jnp.sqrt(sums * SCALE)
 
 
 def solution(mesh):

time: 181 us -> 166 us (0.917)
  Pallas kernels: 173 us -> 160 us
  local copies, waits for them, and re-layouts: 6.08 us -> 2.16 us
  other arithmetic: 1.46 us -> 3.69 us
    pallas_call x1, Pallas kernels: 173 us -> 160 us  [shards(): pl.pallas_call(step_kernel, out_shape=[shape(32, 16, N), shape(6, 32, 16,...]
    unnamed x2 -> x4, local copies, waits for them, and re-layouts: 6 us -> 2.08 us
    mul x0 -> x2, other arithmetic: none -> 2.93 us  [shards(): return (0.5 * result, 0.5 * strain, jnp.sqrt(sums * SCALE))]
where the time goes in v4:
time: 166 us
  Pallas kernels  160 us (96%)
  other arithmetic  3.69 us (2%)
  local copies, waits for them, and re-layouts  2.16 us (1%)
    pallas_call x1, Pallas kernels, shards(): pl.pallas_call(step_kernel, out_shape=[shape(32, 16, N), shape(6, 32, 16,...  160 us

profile of v4, /device:TPU:1, one launch (start us, length us, event | category | flops | bytes accessed | tf_op | source)
XLA Modules:
  0.0 166.1 jit_solution(5005968738329283644)
XLA Ops:
  0.6 0.0 copy-start
  0.6 1.0 copy-done
  1.7 0.0 copy-start.1
  1.7 1.0 copy-done.1
  2.7 159.6 %step.1 = (f32[32,16,256]{2,1,0:T(8,128)S(1)}, f32[6,32,16,256]{3,2,1,0:T(8,128)S(1)}, f32[16,128]{1,0:T(8,128)S(1)}) custom-call(bf16[4,256,256]{2,1,0:T(8,128)(2,1)S(1)} %copy-done.1, f32[32,16,256]{2,1,0:T(8,128)S(1)} %copy-done), custom_call_target="tpu_custom_call" | custom-call | tf_op jit(solution)/shard_map/step/pallas_call | solution.py:799
  162.4 0.8 broadcast_multiply_fusion.1
  163.2 0.1 reduce_sum.10
  163.3 0.1 reduce_sum.14
  163.4 0.1 reduce_sum.18
  163.5 0.5 multiply_sqrt_fusion
  164.0 2.1 %broadcast_multiply_fusion = f32[6,32,16,256]{3,2,1,0:T(8,128)} fusion(f32[6,32,16,256]{3,2,1,0:T(8,128)S(1)} %get-tuple-element.7), kind=kLoop, calls=%fused_computation | loop fusion | flops 786432 | bytes 6291456 | tf_op jit(solution)/shard_map/mul | solution.py:842
Async XLA Ops:
  0.6 1.0 copy-start
  1.7 1.0 copy-start.1

commit v5 on v4

--- a/solution.py
+++ b/solution.py
@@ -186,24 +186,27 @@
 
 def gather_cells(landed, field, wide):
     def go(block, _):
-        for part in range(2):
-            for high in range(2):
-                parts = [landed[field, tile_rows(block, part, high, i), :] for i in range(4)]
-                value = turn_groups(jnp.stack(parts)).reshape(32, H)
-                put_rows(wide, pl.ds(block * 32, 32), part * N + high * H, value)
-        return 0
-
-    lax.fori_loop(0, 8, go, 0)
+        where = [(part, high) for part in range(2) for high in range(2)]
+        tiles = [
+            landed[field, tile_rows(block, part, high, i), :]
+            for part, high in where
+            for i in range(4)
+        ]
+        value = turn_groups(jnp.stack(tiles)).reshape(4, 32, H)
+        for at, (part, high) in enumerate(where):
+            put_rows(wide, pl.ds(block * 32, 32), part * N + high * H, value[at])
+        return 0
+
+    lax.fori_loop(0, 8, go, 0, unroll=2)
 
 
 def scatter_block(out, field, lines, block):
-    for part in range(2):
-        for high in range(2):
-            at = part * N + high * H
-            value = lines[pl.ds(pl.multiple_of(block * 32, 32), 32), at : at + H]
-            value = turn_groups(value.reshape(4, 8, H))
-            for i in range(4):
-                out[field, tile_rows(block, part, high, i), :] = value[i]
+    rows = pl.ds(pl.multiple_of(block * 32, 32), 32)
+    groups = [lines[rows, at * H : (at + 1) * H].reshape(4, 8, H) for at in range(4)]
+    value = turn_groups(jnp.concatenate(groups, axis=0))
+    for at in range(4):
+        for i in range(4):
+            out[field, tile_rows(block, at // 2, at % 2, i), :] = value[at * 4 + i]
 
 
 def signed(index):
@@ -412,6 +415,13 @@
         own = pl.ds(pl.multiple_of(me * 8, 8), 8)
         landed[field, own, :] = sent[field, own, :]
 
+    def send_rows(field, low, high):
+        def go(step, _):
+            send_row(field, step)
+            return 0
+
+        lax.fori_loop(low, high, go, 0)
+
     def send(field):
         send_row(field, 0)
 
@@ -541,15 +551,15 @@
     fill_left(base, xb, -1)
     pl.semaphore_wait(barrier, 127)
     send(PRESSURE)
-    fill_z_back(base, zb)
-    fill_right(base, yb, 1)
-    cells_ahead(CONC, lambda half: cells[half])
-
-    receive(PRESSURE)
     column_send(lambda t: concentration.at[pair_of(t)], plain.at[:, lines_of(col), :], 0)
     plain[:, lines_of(col), :] = concentration[pair_of(col)]
     plain_src, plain_dst = concentration.at[pl.ds(0, 30)], plain.at[:, pl.ds(0, 240), :]
     plain_wait = side_copy(plain_src, plain_dst, 0, (row, next_col))
+    fill_z_back(base, zb)
+    fill_right(base, yb, 1)
+    cells_ahead(CONC, lambda half: cells[half])
+
+    receive(PRESSURE)
     plane_ahead(PRESSURE, 3)
     green_first(spectrum, 3, me)
 
@@ -581,6 +591,8 @@
             def _():
                 if slot in (0, 3, 5):
                     receive(FIRST + field)
+                if slot == 5:
+                    send_rows(CONC, 1, 5)
                 for x in range(2):
                     real, imag = load_plane(landed, FIRST + field, x)
                     if factor is not None:
@@ -670,6 +682,9 @@
         return 0
 
     lax.fori_loop(0, 5, stress_x, 0)
+    send_row(CONC, 0)
+    send_rows(CONC, 5, LINES)
+    keep_own(CONC)
     green_full(spectrum, me)
 
     real_weight = jnp.where(me == 0, 1.0, 2.0) * float(N)
@@ -691,7 +706,6 @@
         return 0
 
     lax.fori_loop(0, 6, shift_back, 0)
-    send(CONC)
 
     col_sums[col, 0:8, :] = fold(partial[0])
     col_sums[col, 8:16, :] = fold(partial[1])

time: 166 us -> 162 us (0.976)
  Pallas kernels: 160 us -> 155 us
    pallas_call x1, Pallas kernels: 160 us -> 155 us  [shards(): pl.pallas_call(step_kernel, out_shape=[shape(32, 16, N), shape(6, 32, 16,...]
where the time goes in v5:
time: 162 us
  Pallas kernels  155 us (96%)
  other arithmetic  3.69 us (2%)
  local copies, waits for them, and re-layouts  2.16 us (1%)
    pallas_call x1, Pallas kernels, shards(): pl.pallas_call(step_kernel, out_shape=[shape(32, 16, N), shape(6, 32, 16,...  155 us

profile of v5, /device:TPU:1, one launch (start us, length us, event | category | flops | bytes accessed | tf_op | source)
XLA Modules:
  0.0 161.5 jit_solution(10034930630911327662)
XLA Ops:
  0.6 0.0 copy-start
  0.6 1.0 copy-done
  1.7 0.0 copy-start.1
  1.7 1.0 copy-done.1
  2.7 155.0 %step.1 = (f32[32,16,256]{2,1,0:T(8,128)S(1)}, f32[6,32,16,256]{3,2,1,0:T(8,128)S(1)}, f32[16,128]{1,0:T(8,128)S(1)}) custom-call(bf16[4,256,256]{2,1,0:T(8,128)(2,1)S(1)} %copy-done.1, f32[32,16,256]{2,1,0:T(8,128)S(1)} %copy-done), custom_call_target="tpu_custom_call" | custom-call | tf_op jit(solution)/shard_map/step/pallas_call | solution.py:813
  157.8 0.8 broadcast_multiply_fusion.1
  158.6 0.1 reduce_sum.10
  158.7 0.1 reduce_sum.14
  158.8 0.1 reduce_sum.18
  158.9 0.5 multiply_sqrt_fusion
  159.5 2.1 %broadcast_multiply_fusion = f32[6,32,16,256]{3,2,1,0:T(8,128)} fusion(f32[6,32,16,256]{3,2,1,0:T(8,128)S(1)} %get-tuple-element.7), kind=kLoop, calls=%fused_computation | loop fusion | flops 786432 | bytes 6291456 | tf_op jit(solution)/shard_map/mul | solution.py:856
Async XLA Ops:
  0.6 1.0 copy-start
  1.7 1.0 copy-start.1
